TPU v7x, 32 devices: a whole 2x2x4 slice. The times are simulated.
32 devices in a mesh: gx: 4 (over y, x), gy: 2 (over core), gz: 4 (over z).
Axes of the slice: x: 2, y: 2, z: 4, core: 2. Of those that a mesh axis runs over, the one named last changes fastest.
Arguments:
- positions: float32 [3, 8, 8, 8, 128], P(None, 'gx', 'gy', 'gz'), may hold values from 0 to 1
- type_ids: int32 [8, 8, 8, 128], P('gx', 'gy', 'gz'), may hold values from 0 to 1
- counts: int32 [8, 8, 8], P('gx', 'gy', 'gz'), may hold values from 64 to 128
- type_charge: float32 [2], replicated, may hold values from -1 to 1
- type_sigma: float32 [2], replicated, may hold values from 0.2 to 0.35
- type_epsilon: float32 [2], replicated, may hold values from 0.05 to 0.5
Outputs:
- forces: float32 [3, 8, 8, 8, 128], P(None, 'gx', 'gy', 'gz')
- totals: float32 [2], replicated
All inputs are finite; a program needn't handle non-finite values.
Results may differ from a plain program's by a relative error of at most 0.0003.
Values sent between devices are 32-bit elements; how exact they have to be, the bound alone decides.
A program may use at most 64 MiB of HBM per device.

v0:
```python
import functools

import jax
import jax.numpy as jnp
from jax import lax
from jax.experimental import pallas as pl
from jax.experimental.pallas import tpu as pltpu
from jax.sharding import PartitionSpec as P

MESH = pl.DeviceIdType.MESH
AXES = ("gx", "gy", "gz")
soft_core = 0.09
cut_sq = 1.0 + soft_core
cut_len = cut_sq**0.5
second_of = {0: (0, 1, 2, 3, 4, 5, 6, 7), 1: (2, 6), 2: (4, 5), 4: (1, 3)}
direct_limit = 64
VMEM_LIMIT = 40 * 1024 * 1024


def corner_of(which):
    return (which & 1, which >> 1 & 1, which >> 2 & 1)


def neighbour(which, step):
    target = {}
    for axis, bit in zip(AXES, corner_of(which)):
        if bit:
            count = lax.axis_size(axis)
            target[axis] = lax.rem(lax.axis_index(axis) + step + count, count)
    return target


def halo_kernel(positions, type_ids, counts, ext, own, send_sem, recv_sem):
    sizes = own.shape[:3]
    width = own.shape[-1]
    barrier = pltpu.get_barrier_semaphore()
    for which in range(1, 8):
        pl.semaphore_signal(barrier, inc=1, device_id=neighbour(which, 1), device_id_type=MESH)
    slot = lax.broadcasted_iota(jnp.int32, (1, width), 1)
    blank = jnp.zeros((4, width), jnp.float32)
    for x in range(sizes[0]):
        for y in range(sizes[1]):
            for z in range(sizes[2]):
                kind = type_ids[x, y, pl.ds(z, 1)].astype(jnp.float32)
                lines = [positions[axis, x, y, pl.ds(z, 1)] for axis in range(3)]
                lines.append(jnp.where(slot < counts[x, y, z], kind, -1.0))
                tile = jnp.concatenate(lines + [blank], 0)
                own[x, y, z] = tile
                ext[x, y, z] = tile
    pl.semaphore_wait(barrier, 7)
    copies = []
    for which in range(1, 8):
        bits = corner_of(which)
        source = tuple(pl.ds(0, 1 if bit else size) for bit, size in zip(bits, sizes))
        target = tuple(
            pl.ds(size, 1) if bit else pl.ds(0, size) for bit, size in zip(bits, sizes)
        )
        copy = pltpu.make_async_remote_copy(
            src_ref=own.at[source],
            dst_ref=ext.at[target],
            send_sem=send_sem.at[which],
            recv_sem=recv_sem.at[which],
            device_id=neighbour(which, -1),
            device_id_type=MESH,
        )
        copy.start()
        copies.append(copy)
    for copy in copies:
        copy.wait()


def type_tables(types, shape, charges, sigmas, epsilons):
    def full(value):
        return jnp.full(shape, value, jnp.float32)

    charge = [full(charges[kind]) for kind in range(types)]
    sigma = [full(sigmas[kind]) for kind in range(types)]
    root = [jnp.sqrt(full(epsilons[kind])) for kind in range(types)]
    tables = {}
    for a in range(types):
        for b in range(types):
            sigma_pair = 0.5 * (sigma[a] + sigma[b])
            depth_pair = 4.0 * root[a] * root[b]
            coulomb = charge[a] * charge[b]
            square = sigma_pair * sigma_pair
            sig_six = square * square * square
            six = 6.0 * depth_pair * sig_six
            twelve = 12.0 * depth_pair * sig_six * sig_six
            cut_six, cut_twelve, cut_coulomb = six * cut_sq**-3, twelve * cut_sq**-6, coulomb / cut_len
            shift = ((cut_six - cut_twelve) - cut_coulomb) / cut_len
            level = cut_len * shift - (cut_twelve / 12.0 - cut_six / 6.0 + cut_coulomb)
            tables[a, b] = (twelve, six, coulomb, shift, level)
    return tables


def pair_kernel(
    types, charges, sigmas, epsilons, ext, reaction, totals,
    rows, first, table, force_i, force_j, held_of,
):
    ext_sizes = ext.shape[:3]
    sizes = tuple(size - 1 for size in ext_sizes)
    width = ext.shape[-1]
    groups = width // 8
    per_cell = 3 + 5 * types
    cells = [
        (x, y, z)
        for x in range(ext_sizes[0])
        for y in range(ext_sizes[1])
        for z in range(ext_sizes[2])
    ]

    def index_of(x, y, z):
        return (x * ext_sizes[1] + y) * ext_sizes[2] + z

    pack = width // 4
    force_j[...] = jnp.zeros(force_j.shape, jnp.float32)
    row_at = lax.broadcasted_iota(jnp.int32, (4, width), 0)
    tables = type_tables(types, (8, width), charges, sigmas, epsilons)
    for cell, (x, y, z) in enumerate(cells):
        base = jnp.where(row_at == 0, x, jnp.where(row_at == 1, y, jnp.where(row_at == 2, z, 0)))
        values = ext[x, y, z, 0:4] + base.astype(jnp.float32)
        held_of[cell] = jnp.sum((values[3:4] >= 0.0).astype(jnp.int32))
        for axis in range(3):
            table[cell, axis] = jnp.broadcast_to(values[axis : axis + 1], (8, width))
        parked = (row_at == 0) & (values[3:4] < 0.0)
        rows[pl.ds(4 * cell, 4)] = jnp.where(parked, x + 4.0, values)
        kind_row = jnp.broadcast_to(values[3:4], (8, width))
        same = [kind_row == float(kind) for kind in range(types)]
        for kind in range(types):
            for at in range(5):
                picked = jnp.zeros((8, width), jnp.float32)
                for second_kind in range(types):
                    picked = jnp.where(same[second_kind], tables[kind, second_kind][at], picked)
                table[cell, 3 + 5 * kind + at] = picked
    for cell, (x, y, z) in enumerate(cells):
        if cell % pack == 0:
            turned = jnp.transpose(rows[pl.ds(4 * cell, width)])
        if (x == sizes[0]) + (y == sizes[1]) + (z == sizes[2]) > 1:
            continue
        for axis in range(4):
            lane = 4 * (cell % pack) + axis
            first[cell, axis] = jnp.broadcast_to(
                turned[:, lane : lane + 1], (width, width)
            ).reshape((groups, 8, width))

    def interact(own, other, kinds, depth, ordered=None):
        xi, yi, zi = own
        second = [table[other, at][None] for at in range(per_cell)]

        def chosen(at):
            value = second[3 + at]
            for kind in range(1, types):
                value = jnp.where(kinds[kind - 1], second[3 + 5 * kind + at], value)
            return value

        dx, dy, dz = second[0] - xi, second[1] - yi, second[2] - zi
        soft_sq = jnp.minimum(dx * dx + dy * dy + dz * dz + soft_core, cut_sq)
        inverse = lax.rsqrt(soft_sq)
        inverse_2 = inverse * inverse
        inverse_6 = inverse_2 * inverse_2 * inverse_2
        twelve = chosen(0) * inverse_6 * inverse_6
        six = chosen(1) * inverse_6
        coulomb = chosen(2) * inverse
        shift = chosen(3) * (soft_sq * inverse)
        slope = ((six - twelve) - (coulomb + shift)) * inverse_2
        forces = (slope * dx, slope * dy, slope * dz)
        if ordered is None:
            for axis in range(3):
                force_j[other, axis] -= jnp.sum(forces[axis], 0)
            return forces, (twelve, six, coulomb, shift)
        value = twelve * (1.0 / 12.0) - six * (1.0 / 6.0) + coulomb - shift + chosen(4)
        return forces, jnp.sum(jnp.where(ordered, value, 0.0), 0)

    def one_cell(member, energy):
        z0 = lax.rem(member, sizes[2])
        y0 = lax.rem(member // sizes[2], sizes[1])
        x0 = member // (sizes[2] * sizes[1])

        def cell_at(which):
            shift = corner_of(which)
            return index_of(x0 + shift[0], y0 + shift[1], z0 + shift[2])

        for first_corner, seconds in second_of.items():
            depth = 2 if first_corner == 0 else 4
            here = cell_at(first_corner)
            others = [cell_at(which) for which in seconds]
            trips = (held_of[here] + (8 * depth - 1)) // (8 * depth)
            part_at = tuple(second_of).index(first_corner)
            slot_at = (
                lax.broadcasted_iota(jnp.int32, (depth, 8, width), 0) * 8
                + lax.broadcasted_iota(jnp.int32, (depth, 8, width), 1)
                - lax.broadcasted_iota(jnp.int32, (depth, 8, width), 2)
            )

            def step(at, carry, first_corner=first_corner, seconds=seconds, depth=depth,
                     here=here, others=others, part_at=part_at, slot_at=slot_at):
                energy, numbers = carry[0], list(carry[1:])
                span = pl.ds(at * depth, depth)
                own = tuple(first[here, axis, span] for axis in range(3))
                kind_at = first[here, 3, span]
                kinds = [kind_at == float(kind) for kind in range(1, types)]
                numbers = [
                    number + jnp.sum(kind.astype(jnp.float32), 0)
                    for number, kind in zip(numbers, kinds)
                ]
                total = None
                sums = None
                for which, other in zip(seconds, others):
                    if which == first_corner:
                        forces, own_energy = interact(
                            own, other, kinds, depth, slot_at + at * (8 * depth) < 0
                        )
                        energy = energy + own_energy
                    else:
                        forces, terms = interact(own, other, kinds, depth)
                        terms = [jnp.sum(term, 0) for term in terms]
                        sums = terms if sums is None else [a + b for a, b in zip(sums, terms)]
                    total = forces if total is None else [a + b for a, b in zip(total, forces)]
                energy = energy + (
                    (sums[0] * (1.0 / 12.0) - sums[1] * (1.0 / 6.0)) + (sums[2] - sums[3])
                )
                for axis in range(3):
                    force_i[part_at, member, axis, span] = total[axis]
                return (energy, *numbers)

            zero = jnp.zeros((8, width), jnp.float32)
            energy, *numbers = lax.fori_loop(
                0, trips, step, (energy,) + (zero,) * (types - 1)
            )
            rest = jnp.full((8, width), (trips * depth).astype(jnp.float32))
            for number in numbers:
                rest = rest - number
            for which, other in zip(seconds, others):
                if which != first_corner:
                    for kind, number in enumerate([rest, *numbers]):
                        energy = energy + number * table[other, 3 + 5 * kind + 4]
        return energy

    members = sizes[0] * sizes[1] * sizes[2]
    energy = lax.fori_loop(0, members, one_cell, jnp.zeros((8, width), jnp.float32))

    virial = jnp.zeros((3, width), jnp.float32)
    ones = jnp.ones((8, 2 * width), jnp.bfloat16)
    reaction[...] = jnp.zeros(reaction.shape, jnp.float32)
    for cell, (x, y, z) in enumerate(cells):
        held = rows[pl.ds(4 * cell + 3, 1)] >= 0.0
        lines = []
        for axis in range(3):
            line = jnp.sum(force_j[cell, axis], 0, keepdims=True)
            partial = None
            for part_at, first_corner in enumerate(second_of):
                spot = [at - bit for at, bit in zip((x, y, z), corner_of(first_corner))]
                if all(0 <= at < size for at, size in zip(spot, sizes)):
                    member = (spot[0] * sizes[1] + spot[1]) * sizes[2] + spot[2]
                    value = force_i[part_at, member, axis].reshape((width, width))
                    partial = value if partial is None else partial + value
            if partial is not None:
                high = partial.astype(jnp.bfloat16)
                low = (partial - high.astype(jnp.float32)).astype(jnp.bfloat16)
                summed = lax.dot_general(
                    ones,
                    jnp.concatenate([high, low], 1),
                    (((1,), (1,)), ((), ())),
                    preferred_element_type=jnp.float32,
                )
                line = line + summed[0:1]
            lines.append(jnp.where(held, line, 0.0))
        force = jnp.concatenate(lines, 0)
        reaction[x, y, z, 0:3] = force
        virial = virial - force * rows[pl.ds(4 * cell, 3)]
    totals[0:1] = jnp.sum(energy, 0, keepdims=True)
    totals[1:2] = jnp.sum(virial, 0, keepdims=True)


def return_kernel(
    normaliser, reaction, part, forces, totals, *scratch
):
    ext_sizes = reaction.shape[:3]
    sizes = tuple(size - 1 for size in ext_sizes)
    landed = scratch[:7]
    send_sem, recv_sem, line, plane, middle, line_send, line_recv, plane_send, plane_recv = scratch[7:]
    count_x, count_y, count_z = (lax.axis_size(axis) for axis in AXES)
    at_x, at_y, at_z = (lax.axis_index(axis) for axis in AXES)
    count_plane = count_y * count_z
    at_plane = at_y * count_z + at_z
    direct = count_x * count_plane <= direct_limit
    if direct:
        count_plane, at_plane = count_x * count_plane, at_x * count_plane + at_plane
        count_x, at_x = 1, 0

    def line_target(step):
        return {"gx": lax.rem(at_x + step, count_x)}

    def plane_target(step):
        spot = lax.rem(at_plane + step, count_plane)
        target = {"gy": lax.rem(spot // count_z, count_y), "gz": lax.rem(spot, count_z)}
        if direct:
            target["gx"] = spot // (count_y * count_z)
        return target

    barrier = pltpu.get_barrier_semaphore()
    for which in range(1, 8):
        pl.semaphore_signal(barrier, inc=1, device_id=neighbour(which, -1), device_id_type=MESH)
    for step in range(1, count_x):
        pl.semaphore_signal(barrier, inc=1, device_id=line_target(step), device_id_type=MESH)
    for step in range(1, count_plane):
        pl.semaphore_signal(barrier, inc=1, device_id=plane_target(step), device_id_type=MESH)
    pl.semaphore_wait(barrier, 7 + count_x - 1 + count_plane - 1)

    def send_plane():
        plane_copies = []
        for step in range(1, count_plane):
            copy = pltpu.make_async_remote_copy(
                src_ref=part if direct else middle,
                dst_ref=plane.at[at_plane],
                send_sem=plane_send.at[step],
                recv_sem=plane_recv.at[step],
                device_id=plane_target(step),
                device_id_type=MESH,
            )
            copy.start()
            plane_copies.append(copy)
        return plane_copies

    copies = []
    for which in range(1, 8):
        source = tuple(
            pl.ds(size, 1) if bit else pl.ds(0, size)
            for bit, size in zip(corner_of(which), sizes)
        )
        copy = pltpu.make_async_remote_copy(
            src_ref=reaction.at[source],
            dst_ref=landed[which - 1],
            send_sem=send_sem.at[which],
            recv_sem=recv_sem.at[which],
            device_id=neighbour(which, 1),
            device_id_type=MESH,
        )
        copy.start()
        copies.append(copy)
    line_copies = []
    for step in range(1, count_x):
        copy = pltpu.make_async_remote_copy(
            src_ref=part,
            dst_ref=line.at[at_x],
            send_sem=line_send.at[step],
            recv_sem=line_recv.at[step],
            device_id=line_target(step),
            device_id_type=MESH,
        )
        copy.start()
        line_copies.append(copy)
    if not direct:
        line[at_x] = part[...]
        for copy in line_copies:
            copy.wait()
        summed = line[0]
        for step in range(1, count_x):
            summed = summed + line[step]
        middle[...] = summed
        plane[at_plane] = summed
    else:
        plane_copies = send_plane()
        plane[at_plane] = part[...]
    for copy in copies:
        copy.wait()
    for x in range(sizes[0]):
        for y in range(sizes[1]):
            for z in range(sizes[2]):
                value = reaction[x, y, z]
                for which in range(1, 8):
                    bits = corner_of(which)
                    spot = (x, y, z)
                    if all(not bit or at == 0 for bit, at in zip(bits, spot)):
                        value = value + landed[which - 1][
                            tuple(0 if bit else at for bit, at in zip(bits, spot))
                        ]
                for axis in range(3):
                    forces[axis, x, y, pl.ds(z, 1)] = value[axis : axis + 1]
    if not direct:
        plane_copies = send_plane()
    for copy in plane_copies:
        copy.wait()
    summed = plane[0]
    for step in range(1, count_plane):
        summed = summed + plane[step]
    totals[0] = jnp.sum(summed[0:1]) * normaliser
    totals[1] = jnp.sum(summed[1:2]) * normaliser


def per_device(positions, type_ids, counts, type_charge, type_sigma, type_epsilon):
    types = type_charge.shape[0]
    sizes, width = type_ids.shape[:3], type_ids.shape[3]
    ext_sizes = tuple(size + 1 for size in sizes)
    cells = ext_sizes[0] * ext_sizes[1] * ext_sizes[2]
    vmem = pl.BlockSpec(memory_space=pltpu.VMEM)
    smem = pl.BlockSpec(memory_space=pltpu.SMEM)
    f32 = jnp.float32
    ext = pl.pallas_call(
        halo_kernel,
        name="halo",
        out_shape=jax.ShapeDtypeStruct(ext_sizes + (8, width), f32),
        in_specs=[vmem, vmem, smem],
        out_specs=vmem,
        scratch_shapes=[pltpu.VMEM(sizes + (8, width), f32), pltpu.SemaphoreType.DMA((8,)), pltpu.SemaphoreType.DMA((8,))],
        compiler_params=pltpu.CompilerParams(
            collective_id=0, has_side_effects=True, vmem_limit_bytes=8 * 1024 * 1024
        ),
    )(positions, type_ids, counts)
    pack = width // 4
    tiles = -(-cells // pack)
    reaction, part = pl.pallas_call(
        functools.partial(pair_kernel, types),
        name="pairs",
        out_shape=(
            jax.ShapeDtypeStruct(ext_sizes + (8, width), f32),
            jax.ShapeDtypeStruct((2, width), f32),
        ),
        in_specs=[smem, smem, smem, vmem],
        out_specs=(vmem, vmem),
        scratch_shapes=[
            pltpu.VMEM((tiles * width, width), f32),
            pltpu.VMEM((cells, 4, width // 8, 8, width), f32),
            pltpu.VMEM((cells, 3 + 5 * types, 8, width), f32),
            pltpu.VMEM(
                (len(second_of), sizes[0] * sizes[1] * sizes[2], 3, width // 8, 8, width), f32
            ),
            pltpu.VMEM((cells, 3, 8, width), f32),
            pltpu.SMEM((cells,), jnp.int32),
        ],
        compiler_params=pltpu.CompilerParams(vmem_limit_bytes=VMEM_LIMIT),
    )(type_charge, type_sigma, type_epsilon, ext)
    count_x, count_y, count_z = (lax.axis_size(axis) for axis in AXES)
    count_plane = count_y * count_z
    slots_x, slots_plane = count_x, count_plane
    if count_x * count_plane <= direct_limit:
        slots_x, slots_plane = 1, count_x * count_plane
    normaliser = 1.0 / (
        sizes[0] * count_x * sizes[1] * count_y * sizes[2] * count_z * width
    )
    landing = [
        pltpu.VMEM(
            tuple(1 if bit else size for bit, size in zip(corner_of(which), sizes)) + (8, width),
            f32,
        )
        for which in range(1, 8)
    ]
    forces, totals = pl.pallas_call(
        functools.partial(return_kernel, normaliser),
        name="giveback",
        out_shape=(
            jax.ShapeDtypeStruct((3,) + sizes + (width,), f32),
            jax.ShapeDtypeStruct((2,), f32),
        ),
        in_specs=[vmem, vmem],
        out_specs=(vmem, smem),
        scratch_shapes=landing
        + [
            pltpu.SemaphoreType.DMA((8,)),
            pltpu.SemaphoreType.DMA((8,)),
            pltpu.VMEM((slots_x, 2, width), f32),
            pltpu.VMEM((slots_plane, 2, width), f32),
            pltpu.VMEM((2, width), f32),
            pltpu.SemaphoreType.DMA((slots_x,)),
            pltpu.SemaphoreType.DMA((slots_x,)),
            pltpu.SemaphoreType.DMA((slots_plane,)),
            pltpu.SemaphoreType.DMA((slots_plane,)),
        ],
        compiler_params=pltpu.CompilerParams(
            collective_id=1, has_side_effects=True, vmem_limit_bytes=8 * 1024 * 1024
        ),
    )(reaction, part)
    return forces, totals


def solution(mesh):
    in_specs = (
        P(None, "gx", "gy", "gz", None),
        P("gx", "gy", "gz", None),
        P("gx", "gy", "gz"),
        P(),
        P(),
        P(),
    )
    out_specs = (P(None, "gx", "gy", "gz", None), P())
    return jax.shard_map(
        per_device, mesh=mesh, in_specs=in_specs, out_specs=out_specs, check_vma=False
    )
```

profile of v0, /device:TPU:0, one launch (start us, length us, event | category | flops | bytes accessed | tf_op | source)
XLA Modules:
  0.0 51.6 jit_solution(2707478176668031865)
XLA Ops:
  0.6 0.8 %copy.8.counts = s32[2,4,2]{2,1,0:T(4,128)S(1)} copy(s32[2,4,2]{1,2,0:T(2,128)} %param.8) | data formatting | bytes 128 | tf_op args[2]
  1.4 0.0 copy-start
  1.4 0.7 %copy-done = f32[3,2,4,2,128]{4,3,2,1,0:T(2,128)S(1)} copy-done((f32[3,2,4,2,128]{4,3,2,1,0:T(2,128)S(1)}, f32[3,2,4,2,128]{4,3,2,1,0:T(2,128)}, u32[]{:S(2)}) %copy-start) | copy-done | bytes 24600
  2.1 0.0 copy-start.1
  2.1 0.7 %copy-done.1 = s32[2,4,2,128]{3,2,1,0:T(2,128)S(1)} copy-done((s32[2,4,2,128]{3,2,1,0:T(2,128)S(1)}, s32[2,4,2,128]{3,2,1,0:T(2,128)}, u32[]{:S(2)}) %copy-start.1) | copy-done | bytes 8216
  2.8 0.0 copy-start.2
  2.8 0.0 copy-start.3
  2.8 0.0 copy-start.4
  2.8 9.6 %halo.1.ext = f32[3,5,3,8,128]{4,3,2,1,0:T(8,128)S(1)} custom-call(f32[3,2,4,2,128]{4,3,2,1,0:T(2,128)S(1)} %copy-done, s32[2,4,2,128]{3,2,1,0:T(2,128)S(1)} %copy-done.1, s32[2,4,2]{2,1,0:T(4,128)S(1)} %copy.8.counts), custom_call_target="tpu_custom_call" | custom-call | tf_op jit(solution)/shard_map/halo/pallas_call | solution.py:399
  12.5 0.0 copy-done.2
  12.5 0.0 copy-done.3
  12.5 0.0 copy-done.4
  12.5 26.8 %pairs.1 = (f32[3,5,3,8,128]{4,3,2,1,0:T(8,128)S(1)}, f32[2,128]{1,0:T(2,128)S(1)}) custom-call(f32[2]{0:T(128)S(1)} %copy-done.2, f32[2]{0:T(128)S(1)} %copy-done.3, f32[2]{0:T(128)S(1)} %copy-done.4, f32[3,5,3,8,128]{4,3,2,1,0:T(8,128)S(1)} %halo.1.ext), custom_call_target="tpu_custom_call" | custom-call | tf_op jit(solution)/shard_map/pairs/pallas_call | solution.py:412
  39.3 11.1 %giveback.1 = (f32[3,2,4,2,128]{4,3,2,1,0:T(2,128)S(1)}, f32[2]{0:T(128)S(1)}) custom-call(f32[3,5,3,8,128]{4,3,2,1,0:T(8,128)S(1)} %get-tuple-element.4.reaction, f32[2,128]{1,0:T(2,128)S(1)} %get-tuple-element.5.part), custom_call_target="tpu_custom_call" | custom-call | tf_op jit(solution)/shard_map/giveback/pallas_call | solution.py:448
  50.4 0.6 %copy.11 = f32[3,2,4,2,128]{4,3,2,1,0:T(2,128)} copy(f32[3,2,4,2,128]{4,3,2,1,0:T(2,128)S(1)} %get-tuple-element.8) | data formatting | bytes 49152
  51.1 0.5 copy.12
Async XLA Ops:
  1.4 0.7 %copy-start = (f32[3,2,4,2,128]{4,3,2,1,0:T(2,128)S(1)}, f32[3,2,4,2,128]{4,3,2,1,0:T(2,128)}, u32[]{:S(2)}) copy-start(f32[3,2,4,2,128]{4,3,2,1,0:T(2,128)} %positions.1) | copy-start | bytes 73732
  2.1 0.7 %copy-start.1 = (s32[2,4,2,128]{3,2,1,0:T(2,128)S(1)}, s32[2,4,2,128]{3,2,1,0:T(2,128)}, u32[]{:S(2)}) copy-start(s32[2,4,2,128]{3,2,1,0:T(2,128)} %type_ids.1) | copy-start | bytes 24580
  2.8 9.6 %copy-start.2 = (f32[2]{0:T(128)S(1)}, f32[2]{0:T(128)}, u32[]{:S(2)}) copy-start(f32[2]{0:T(128)} %charges.1) | copy-start | bytes 28
  2.8 9.6 %copy-start.3 = (f32[2]{0:T(128)S(1)}, f32[2]{0:T(128)}, u32[]{:S(2)}) copy-start(f32[2]{0:T(128)} %sigmas.1) | copy-start | bytes 28
  2.8 9.7 %copy-start.4 = (f32[2]{0:T(128)S(1)}, f32[2]{0:T(128)}, u32[]{:S(2)}) copy-start(f32[2]{0:T(128)} %epsilons.1) | copy-start | bytes 28
where the time goes:
time: 52 us; the launch traced here: 51.6 us
  Pallas kernels  47.5 us (91%)
  local copies, waits for them, and re-layouts  3.34 us (6%)
  between operations  0.68 us (1%)
    pallas_call x1, Pallas kernels, per_device(): pl.pallas_call(functools.partial(pair_kernel, types), name='pairs', out_s...  26.8 us
    pallas_call x1, Pallas kernels, per_device(): pl.pallas_call(functools.partial(return_kernel, normaliser), name='giveba...  11.1 us
    pallas_call x1, Pallas kernels, per_device(): pl.pallas_call(halo_kernel, name='halo', out_shape=jax.ShapeDtypeStruct(e...  9.62 us
    unnamed x13, local copies, waits for them, and re-layouts  3.34 us

commit v1 on v0

v1 whole, which is shorter than its diff:
```python
import functools

import jax
import jax.numpy as jnp
from jax import lax
from jax.experimental import pallas as pl
from jax.experimental.pallas import tpu as pltpu
from jax.sharding import PartitionSpec as P

MESH = pl.DeviceIdType.MESH
AXES = ("gx", "gy", "gz")
soft_core = 0.09
cut_sq = 1.0 + soft_core
cut_len = cut_sq**0.5
second_of = {0: (0, 1, 2, 3, 4, 5, 6, 7), 1: (2, 6), 2: (4, 5), 4: (1, 3)}
direct_limit = 64
VMEM_LIMIT = 56 * 1024 * 1024


def corner_of(which):
    return (which & 1, which >> 1 & 1, which >> 2 & 1)


def neighbour(which, step):
    target = {}
    for axis, bit in zip(AXES, corner_of(which)):
        if bit:
            count = lax.axis_size(axis)
            target[axis] = lax.rem(lax.axis_index(axis) + step + count, count)
    return target


def type_tables(types, shape, charges, sigmas, epsilons):
    def full(value):
        return jnp.full(shape, value, jnp.float32)

    charge = [full(charges[kind]) for kind in range(types)]
    sigma = [full(sigmas[kind]) for kind in range(types)]
    root = [jnp.sqrt(full(epsilons[kind])) for kind in range(types)]
    tables = {}
    for a in range(types):
        for b in range(types):
            sigma_pair = 0.5 * (sigma[a] + sigma[b])
            depth_pair = 4.0 * root[a] * root[b]
            coulomb = charge[a] * charge[b]
            square = sigma_pair * sigma_pair
            sig_six = square * square * square
            six = 6.0 * depth_pair * sig_six
            twelve = 12.0 * depth_pair * sig_six * sig_six
            cut_six, cut_twelve, cut_coulomb = six * cut_sq**-3, twelve * cut_sq**-6, coulomb / cut_len
            shift = ((cut_six - cut_twelve) - cut_coulomb) / cut_len
            level = cut_len * shift - (cut_twelve / 12.0 - cut_six / 6.0 + cut_coulomb)
            tables[a, b] = (twelve, six, coulomb, shift, level)
    return tables


def step_kernel(
    normaliser, types, charges, sigmas, epsilons, positions, type_ids, counts, forces, totals,
    place_in, kind_in, count_in, own, ext, rows, first, table, number_of, force_i, force_j, react, part,
    in_sem, halo_send, halo_recv, back_send, back_recv,
    line, plane, middle, line_send, line_recv, plane_send, plane_recv, *landed,
):
    sizes = own.shape[:3]
    ext_sizes = ext.shape[:3]
    width = own.shape[-1]
    groups = width // 8
    per_cell = 3 + 5 * types
    members = sizes[0] * sizes[1] * sizes[2]
    count_x, count_y, count_z = (lax.axis_size(axis) for axis in AXES)
    at_x, at_y, at_z = (lax.axis_index(axis) for axis in AXES)
    count_plane = count_y * count_z
    at_plane = at_y * count_z + at_z
    direct = count_x * count_plane <= direct_limit
    if direct:
        count_plane, at_plane = count_x * count_plane, at_x * count_plane + at_plane
        count_x, at_x = 1, 0

    def line_target(step):
        return {"gx": lax.rem(at_x + step, count_x)}

    def plane_target(step):
        spot = lax.rem(at_plane + step, count_plane)
        target = {"gy": lax.rem(spot // count_z, count_y), "gz": lax.rem(spot, count_z)}
        if direct:
            target["gx"] = spot // (count_y * count_z)
        return target

    barrier = pltpu.get_barrier_semaphore()
    greeted = count_x - 1 + count_plane - 1
    if not direct:
        greeted += 14
        for which in range(1, 8):
            for step in (1, -1):
                pl.semaphore_signal(barrier, inc=1, device_id=neighbour(which, step), device_id_type=MESH)
    for step in range(1, count_x):
        pl.semaphore_signal(barrier, inc=1, device_id=line_target(step), device_id_type=MESH)
    for step in range(1, count_plane):
        pl.semaphore_signal(barrier, inc=1, device_id=plane_target(step), device_id_type=MESH)

    loads = [
        pltpu.make_async_copy(source, target, in_sem.at[at])
        for at, (source, target) in enumerate(
            ((positions, place_in), (type_ids, kind_in), (counts, count_in))
        )
    ]
    for load in loads:
        load.start()

    cells = [
        (x, y, z)
        for x in range(ext_sizes[0])
        for y in range(ext_sizes[1])
        for z in range(ext_sizes[2])
    ]

    def outside(cell):
        return sum(at == size for at, size in zip(cell, sizes))

    def index_of(x, y, z):
        return (x * ext_sizes[1] + y) * ext_sizes[2] + z

    ordered = sorted(cells, key=outside)
    row_of = {cell: 4 * at for at, cell in enumerate(ordered)}
    inner = [cell for cell in ordered if outside(cell) == 0]
    outer = [cell for cell in ordered if outside(cell) > 0]

    tables = type_tables(types, (8, width), charges, sigmas, epsilons)
    force_j[...] = jnp.zeros(force_j.shape, jnp.float32)
    react[...] = jnp.zeros(react.shape, jnp.float32)
    row_at = lax.broadcasted_iota(jnp.int32, (4, width), 0)
    slot = lax.broadcasted_iota(jnp.int32, (1, width), 1)

    for load in loads:
        load.wait()
    for x, y, z in inner:
        lines = [place_in[axis, x, y, pl.ds(z, 1)] for axis in range(3)]
        kind = kind_in[x, y, pl.ds(z, 1)].astype(jnp.float32)
        held = jnp.broadcast_to(count_in[x, pl.ds(z, 1), pl.ds(y, 1)], (1, width))
        lines.append(jnp.where(slot < held, kind, -1.0))
        tile = jnp.concatenate(lines, 0)
        own[x, y, z] = tile
        ext[x, y, z] = tile

    def build(some):
        for x, y, z in some:
            cell = index_of(x, y, z)
            base = jnp.where(row_at == 0, x, jnp.where(row_at == 1, y, jnp.where(row_at == 2, z, 0)))
            values = ext[x, y, z] + base.astype(jnp.float32)
            for axis in range(3):
                table[cell, axis] = jnp.broadcast_to(values[axis : axis + 1], (8, width))
            parked = (row_at == 0) & (values[3:4] < 0.0)
            rows[pl.ds(row_of[x, y, z], 4)] = jnp.where(parked, x + 4.0, values)
            kind_row = jnp.broadcast_to(values[3:4], (8, width))
            same = [kind_row == float(kind) for kind in range(types)]
            for kind in range(types):
                for at in range(5):
                    picked = jnp.zeros((8, width), jnp.float32)
                    for second_kind in range(types):
                        picked = jnp.where(same[second_kind], tables[kind, second_kind][at], picked)
                    table[cell, 3 + 5 * kind + at] = picked
        leading = [cell for cell in some if outside(cell) <= 1]
        pack = width // 4
        for start in range(0, len(leading), pack):
            batch = leading[start : start + pack]
            turned = jnp.transpose(rows[pl.ds(row_of[batch[0]], width)])
            for at, (x, y, z) in enumerate(batch):
                cell = index_of(x, y, z)
                for axis in range(4):
                    lane = 4 * at + axis
                    spread = jnp.broadcast_to(
                        turned[:, lane : lane + 1], (width, width)
                    ).reshape((groups, 8, width))
                    first[cell, axis] = spread
                for kind in range(1, types):
                    number_of[cell, kind - 1] = jnp.sum((spread == float(kind)).astype(jnp.float32), 0)

    build(inner)

    def interact(own_at, other, kinds, ordered=None):
        xi, yi, zi = own_at
        second = [table[other, at][None] for at in range(per_cell)]

        def chosen(at):
            value = second[3 + at]
            for kind in range(1, types):
                value = jnp.where(kinds[kind - 1], second[3 + 5 * kind + at], value)
            return value

        dx, dy, dz = second[0] - xi, second[1] - yi, second[2] - zi
        soft_sq = jnp.minimum(dx * dx + dy * dy + dz * dz + soft_core, cut_sq)
        inverse = lax.rsqrt(soft_sq)
        inverse_2 = inverse * inverse
        inverse_6 = inverse_2 * inverse_2 * inverse_2
        twelve = chosen(0) * inverse_6 * inverse_6
        six = chosen(1) * inverse_6
        coulomb = chosen(2) * inverse
        shift = chosen(3) * (soft_sq * inverse)
        slope = ((six - twelve) - (coulomb + shift)) * inverse_2
        forces = (slope * dx, slope * dy, slope * dz)
        if ordered is None:
            for axis in range(3):
                force_j[other, axis] -= jnp.sum(forces[axis], 0)
            return forces, (twelve, six, coulomb, shift)
        value = twelve * (1.0 / 12.0) - six * (1.0 / 6.0) + coulomb - shift + chosen(4)
        return forces, jnp.sum(jnp.where(ordered, value, 0.0), 0)

    def role(first_corner, seconds, member, cell_at, energy, depth):
        here = cell_at(first_corner)
        others = [cell_at(which) for which in seconds]
        part_at = tuple(second_of).index(first_corner) + (1 if seconds[0] else 0)
        trips = groups // depth
        slot_at = (
            lax.broadcasted_iota(jnp.int32, (depth, 8, width), 0) * 8
            + lax.broadcasted_iota(jnp.int32, (depth, 8, width), 1)
            - lax.broadcasted_iota(jnp.int32, (depth, 8, width), 2)
        )

        def step(at, energy):
            span = pl.ds(at * depth, depth)
            own_at = tuple(first[here, axis, span] for axis in range(3))
            kind_at = first[here, 3, span]
            kinds = [kind_at == float(kind) for kind in range(1, types)]
            total = None
            sums = None
            for which, other in zip(seconds, others):
                if which == first_corner:
                    forces, own_energy = interact(
                        own_at, other, kinds, slot_at + at * (8 * depth) < 0
                    )
                    energy = energy + own_energy
                else:
                    forces, terms = interact(own_at, other, kinds)
                    terms = [jnp.sum(term, 0) for term in terms]
                    sums = terms if sums is None else [a + b for a, b in zip(sums, terms)]
                total = forces if total is None else [a + b for a, b in zip(total, forces)]
            if sums is not None:
                energy = energy + (
                    (sums[0] * (1.0 / 12.0) - sums[1] * (1.0 / 6.0)) + (sums[2] - sums[3])
                )
            for axis in range(3):
                force_i[part_at, member, axis, span] = total[axis]
            return energy

        energy = lax.fori_loop(0, trips, step, energy)
        for which, other in zip(seconds, others):
            if which != first_corner:
                numbers = [number_of[here, kind - 1] for kind in range(1, types)]
                rest = jnp.full((8, width), float(groups))
                for number in numbers:
                    rest = rest - number
                for kind, number in enumerate([rest, *numbers]):
                    energy = energy + number * table[other, 3 + 5 * kind + 4]
        return energy

    def corners(x0, y0, z0):
        def cell_at(which):
            shift = corner_of(which)
            return index_of(x0 + shift[0], y0 + shift[1], z0 + shift[2])

        return cell_at

    def one_self(member, energy):
        z0 = lax.rem(member, sizes[2])
        y0 = lax.rem(member // sizes[2], sizes[1])
        x0 = member // (sizes[2] * sizes[1])
        return role(0, (0,), member, corners(x0, y0, z0), energy, 4)

    def across(x0, y0, z0, energy):
        member = (x0 * sizes[1] + y0) * sizes[2] + z0
        cell_at = corners(x0, y0, z0)
        for first_corner, seconds in second_of.items():
            seconds = tuple(which for which in seconds if which)
            energy = role(first_corner, seconds, member, cell_at, energy, 2 if first_corner == 0 else 4)
        return energy

    energy = lax.fori_loop(0, members, one_self, jnp.zeros((8, width), jnp.float32))

    pl.semaphore_wait(barrier, greeted)
    halos = []
    for which in range(1, 8):
        bits = corner_of(which)
        source = tuple(pl.ds(0, 1 if bit else size) for bit, size in zip(bits, sizes))
        target = tuple(
            pl.ds(size, 1) if bit else pl.ds(0, size) for bit, size in zip(bits, sizes)
        )
        copy = pltpu.make_async_remote_copy(
            src_ref=own.at[source],
            dst_ref=ext.at[target],
            send_sem=halo_send.at[which],
            recv_sem=halo_recv.at[which],
            device_id=neighbour(which, -1),
            device_id_type=MESH,
        )
        copy.start()
        halos.append(copy)

    less = tuple(size - 1 for size in sizes)

    def inside(at, energy):
        z0 = lax.rem(at, less[2])
        y0 = lax.rem(at // less[2], less[1])
        x0 = at // (less[2] * less[1])
        return across(x0, y0, z0, energy)

    if less[0] * less[1] * less[2]:
        energy = lax.fori_loop(0, less[0] * less[1] * less[2], inside, energy)

    for copy in halos:
        copy.wait()
    build(outer)

    sheet, bar = sizes[1] * sizes[2], less[0] * sizes[2]

    def border(at, energy):
        at_sheet, at_bar, at_rest = at, at - sheet, at - sheet - bar
        on_sheet, on_bar = at < sheet, at < sheet + bar
        x0 = jnp.where(on_sheet, less[0], jnp.where(on_bar, at_bar // sizes[2], at_rest // max(less[1], 1)))
        y0 = jnp.where(on_sheet, at_sheet // sizes[2], jnp.where(on_bar, less[1], lax.rem(at_rest, max(less[1], 1))))
        z0 = jnp.where(on_sheet | on_bar, lax.rem(jnp.where(on_sheet, at_sheet, at_bar), sizes[2]), less[2])
        return across(x0, y0, z0, energy)

    energy = lax.fori_loop(0, sheet + bar + less[0] * less[1], border, energy)

    virial = jnp.zeros((3, width), jnp.float32)

    def reduced(cell):
        x, y, z = cell
        at_cell = index_of(x, y, z)
        held = rows[pl.ds(row_of[cell] + 3, 1)] >= 0.0
        lines = []
        for axis in range(3):
            line = force_j[at_cell, axis]
            partial = None
            for part_at, first_corner in enumerate((0, 0, 1, 2, 4)):
                spot = [at - bit for at, bit in zip(cell, corner_of(first_corner))]
                if all(0 <= at < size for at, size in zip(spot, sizes)):
                    member = (spot[0] * sizes[1] + spot[1]) * sizes[2] + spot[2]
                    value = force_i[part_at, member, axis].reshape((width, width))
                    partial = value if partial is None else partial + value
            if partial is not None:
                turned = jnp.transpose(partial)
                line = line + jnp.sum(turned.reshape((groups, 8, width)), 0)
            line = jnp.sum(line, 0, keepdims=True)
            lines.append(jnp.where(held, line, 0.0))
        return jnp.concatenate(lines, 0)

    for cell in outer:
        force = reduced(cell)
        react[cell[0], cell[1], cell[2], 0:3] = force
        virial = virial - force * rows[pl.ds(row_of[cell], 3)]
    backs = []
    for which in range(1, 8):
        source = tuple(
            pl.ds(size, 1) if bit else pl.ds(0, size)
            for bit, size in zip(corner_of(which), sizes)
        )
        copy = pltpu.make_async_remote_copy(
            src_ref=react.at[source],
            dst_ref=landed[which - 1],
            send_sem=back_send.at[which],
            recv_sem=back_recv.at[which],
            device_id=neighbour(which, 1),
            device_id_type=MESH,
        )
        copy.start()
        backs.append(copy)
    for cell in inner:
        force = reduced(cell)
        react[cell[0], cell[1], cell[2], 0:3] = force
        virial = virial - force * rows[pl.ds(row_of[cell], 3)]
    part[0:1] = jnp.sum(energy, 0, keepdims=True)
    part[1:2] = jnp.sum(virial, 0, keepdims=True)

    def send_plane():
        plane_copies = []
        for step in range(1, count_plane):
            copy = pltpu.make_async_remote_copy(
                src_ref=part if direct else middle,
                dst_ref=plane.at[at_plane],
                send_sem=plane_send.at[step],
                recv_sem=plane_recv.at[step],
                device_id=plane_target(step),
                device_id_type=MESH,
            )
            copy.start()
            plane_copies.append(copy)
        return plane_copies

    if direct:
        plane_copies = send_plane()
        plane[at_plane] = part[...]
    else:
        line_copies = []
        for step in range(1, count_x):
            copy = pltpu.make_async_remote_copy(
                src_ref=part,
                dst_ref=line.at[at_x],
                send_sem=line_send.at[step],
                recv_sem=line_recv.at[step],
                device_id=line_target(step),
                device_id_type=MESH,
            )
            copy.start()
            line_copies.append(copy)
        line[at_x] = part[...]
        for copy in line_copies:
            copy.wait()
        summed = line[0]
        for step in range(1, count_x):
            summed = summed + line[step]
        middle[...] = summed
        plane[at_plane] = summed
        plane_copies = send_plane()
    for copy in backs:
        copy.wait()
    for x, y, z in inner:
        value = react[x, y, z]
        for which in range(1, 8):
            bits = corner_of(which)
            spot = (x, y, z)
            if all(not bit or at == 0 for bit, at in zip(bits, spot)):
                value = value + landed[which - 1][
                    tuple(0 if bit else at for bit, at in zip(bits, spot))
                ]
        for axis in range(3):
            forces[axis, x, y, pl.ds(z, 1)] = value[axis : axis + 1]
    for copy in plane_copies:
        copy.wait()
    summed = plane[0]
    for step in range(1, count_plane):
        summed = summed + plane[step]
    totals[0] = jnp.sum(summed[0:1]) * normaliser
    totals[1] = jnp.sum(summed[1:2]) * normaliser


def per_device(positions, type_ids, counts, type_charge, type_sigma, type_epsilon):
    types = type_charge.shape[0]
    sizes, width = type_ids.shape[:3], type_ids.shape[3]
    ext_sizes = tuple(size + 1 for size in sizes)
    cells = ext_sizes[0] * ext_sizes[1] * ext_sizes[2]
    members = sizes[0] * sizes[1] * sizes[2]
    vmem = pl.BlockSpec(memory_space=pltpu.VMEM)
    smem = pl.BlockSpec(memory_space=pltpu.SMEM)
    hbm = pl.BlockSpec(memory_space=pltpu.HBM)
    f32 = jnp.float32
    count_x, count_y, count_z = (lax.axis_size(axis) for axis in AXES)
    count_plane = count_y * count_z
    slots_x, slots_plane = count_x, count_plane
    if count_x * count_plane <= direct_limit:
        slots_x, slots_plane = 1, count_x * count_plane
    normaliser = 1.0 / (
        sizes[0] * count_x * sizes[1] * count_y * sizes[2] * count_z * width
    )
    landing = [
        pltpu.VMEM(
            tuple(1 if bit else size for bit, size in zip(corner_of(which), sizes)) + (4, width),
            f32,
        )
        for which in range(1, 8)
    ]
    counts = jnp.transpose(counts, (0, 2, 1))
    dma = pltpu.SemaphoreType.DMA
    return pl.pallas_call(
        functools.partial(step_kernel, normaliser, types),
        name="step",
        out_shape=(
            jax.ShapeDtypeStruct((3,) + sizes + (width,), f32),
            jax.ShapeDtypeStruct((2,), f32),
        ),
        in_specs=[smem, smem, smem, hbm, hbm, hbm],
        out_specs=(vmem, smem),
        scratch_shapes=[
            pltpu.VMEM(positions.shape, f32),
            pltpu.VMEM(type_ids.shape, jnp.int32),
            pltpu.VMEM(counts.shape, jnp.int32),
            pltpu.VMEM(sizes + (4, width), f32),
            pltpu.VMEM(ext_sizes + (4, width), f32),
            pltpu.VMEM((4 * cells + width, width), f32),
            pltpu.VMEM((cells, 4, width // 8, 8, width), f32),
            pltpu.VMEM((cells, 3 + 5 * types, 8, width), f32),
            pltpu.VMEM((cells, types - 1, 8, width), f32),
            pltpu.VMEM((1 + len(second_of), members, 3, width // 8, 8, width), f32),
            pltpu.VMEM((cells, 3, 8, width), f32),
            pltpu.VMEM(ext_sizes + (4, width), f32),
            pltpu.VMEM((2, width), f32),
            dma((3,)),
            dma((8,)),
            dma((8,)),
            dma((8,)),
            dma((8,)),
            pltpu.VMEM((slots_x, 2, width), f32),
            pltpu.VMEM((slots_plane, 2, width), f32),
            pltpu.VMEM((2, width), f32),
            dma((slots_x,)),
            dma((slots_x,)),
            dma((slots_plane,)),
            dma((slots_plane,)),
        ]
        + landing,
        compiler_params=pltpu.CompilerParams(
            collective_id=0, has_side_effects=True, vmem_limit_bytes=VMEM_LIMIT
        ),
    )(type_charge, type_sigma, type_epsilon, positions, type_ids, counts)


def solution(mesh):
    in_specs = (
        P(None, "gx", "gy", "gz", None),
        P("gx", "gy", "gz", None),
        P("gx", "gy", "gz"),
        P(),
        P(),
        P(),
    )
    out_specs = (P(None, "gx", "gy", "gz", None), P())
    return jax.shard_map(
        per_device, mesh=mesh, in_specs=in_specs, out_specs=out_specs, check_vma=False
    )
```

time: 52 us -> 45.1 us (0.87)
  Pallas kernels: 47.5 us -> 42.3 us
  local copies, waits for them, and re-layouts: 3.34 us -> 1.86 us
    pallas_call x3 -> x1, Pallas kernels: 47.5 us -> 42.3 us  [per_device(): pl.pallas_call(functools.partial(step_kernel, normaliser, types), name='s...]
    unnamed x13 -> x4, local copies, waits for them, and re-layouts: 3.34 us -> 1.86 us
where the time goes in v1:
time: 45.1 us; the launch traced here: 44.9 us
  Pallas kernels  42.3 us (94%)
  local copies, waits for them, and re-layouts  1.86 us (4%)
  between operations  0.65 us (1%)
    pallas_call x1, Pallas kernels, per_device(): pl.pallas_call(functools.partial(step_kernel, normaliser, types), name='s...  42.3 us
    unnamed x4, local copies, waits for them, and re-layouts  1.86 us

profile of v1, /device:TPU:0, one launch (start us, length us, event | category | flops | bytes accessed | tf_op | source)
XLA Modules:
  0.0 44.9 jit_solution(9916832832942708204)
XLA Ops:
  0.6 42.3 %step.1 = (f32[3,2,4,2,128]{4,3,2,1,0:T(2,128)}, f32[2]{0:T(128)}) custom-call(f32[2]{0:T(128)} %charges.1, f32[2]{0:T(128)} %sigmas.1, f32[2]{0:T(128)} %epsilons.1, f32[3,2,4,2,128]{4,3,2,1,0:T(2,128)} %positions.1, s32[2,4,2,128]{3,2,1,0:T(2,128)} %type_ids.1, s32[2,2,4]{2,1,0:T(2,128)} %bitcast.1), custom_call_target="tpu_custom_call" | custom-call | tf_op jit(solution)/shard_map/step/pallas_call | solution.py:463
  43.0 0.0 copy-start
  43.0 1.3 %copy.10 = f32[3,2,4,2,128]{4,3,2,1,0:T(2,128)} copy(f32[3,2,4,2,128]{4,3,2,1,0:T(2,128)} %get-tuple-element.4) | data formatting | bytes 49152
  44.3 0.0 copy-done
  44.3 0.5 %copy.11 = f32[2]{0:T(128)} copy(f32[2]{0:T(128)S(1)} %copy-done) | data formatting | bytes 16
Async XLA Ops:
  43.0 1.4 %copy-start = (f32[2]{0:T(128)S(1)}, f32[2]{0:T(128)}, u32[]{:S(2)}) copy-start(f32[2]{0:T(128)} %get-tuple-element.5) | copy-start | bytes 28

commit v2 on v1

--- a/solution.py
+++ b/solution.py
@@ -56,7 +56,7 @@
 
 def step_kernel(
     normaliser, types, charges, sigmas, epsilons, positions, type_ids, counts, forces, totals,
-    place_in, kind_in, count_in, own, ext, rows, first, table, number_of, force_i, force_j, react, part,
+    place_in, kind_in, count_in, own, ext, rows, turn, first, table, number_of, force_i, force_j, react, part,
     in_sem, halo_send, halo_recv, back_send, back_recv,
     line, plane, middle, line_send, line_recv, plane_send, plane_recv, *landed,
 ):
@@ -71,18 +71,30 @@
     count_plane = count_y * count_z
     at_plane = at_y * count_z + at_z
     direct = count_x * count_plane <= direct_limit
+    loads = [
+        pltpu.make_async_copy(source, target, in_sem.at[at])
+        for at, (source, target) in enumerate(
+            ((positions, place_in), (type_ids, kind_in), (counts, count_in))
+        )
+    ]
+    for load in loads:
+        load.start()
+
+    def around(at, count):
+        return [at] + [at + step - count * (at + step >= count).astype(jnp.int32) for step in range(1, count)]
+
+    spots = [around(at, count) for at, count in ((at_x, count_x), (at_y, count_y), (at_z, count_z))]
     if direct:
         count_plane, at_plane = count_x * count_plane, at_x * count_plane + at_plane
         count_x, at_x = 1, 0
 
     def line_target(step):
-        return {"gx": lax.rem(at_x + step, count_x)}
+        return {"gx": spots[0][step]}
 
     def plane_target(step):
-        spot = lax.rem(at_plane + step, count_plane)
-        target = {"gy": lax.rem(spot // count_z, count_y), "gz": lax.rem(spot, count_z)}
+        target = {"gy": spots[1][step // count_z % count_y], "gz": spots[2][step % count_z]}
         if direct:
-            target["gx"] = spot // (count_y * count_z)
+            target["gx"] = spots[0][step // (count_y * count_z)]
         return target
 
     barrier = pltpu.get_barrier_semaphore()
@@ -97,15 +109,6 @@
     for step in range(1, count_plane):
         pl.semaphore_signal(barrier, inc=1, device_id=plane_target(step), device_id_type=MESH)
 
-    loads = [
-        pltpu.make_async_copy(source, target, in_sem.at[at])
-        for at, (source, target) in enumerate(
-            ((positions, place_in), (type_ids, kind_in), (counts, count_in))
-        )
-    ]
-    for load in loads:
-        load.start()
-
     cells = [
         (x, y, z)
         for x in range(ext_sizes[0])
@@ -152,6 +155,9 @@
             rows[pl.ds(row_of[x, y, z], 4)] = jnp.where(parked, x + 4.0, values)
             kind_row = jnp.broadcast_to(values[3:4], (8, width))
             same = [kind_row == float(kind) for kind in range(types)]
+            for kind in range(1, types):
+                total = jnp.sum(same[kind].astype(jnp.float32), 1, keepdims=True) * 0.125
+                number_of[cell, kind - 1] = jnp.broadcast_to(total, (8, width))
             for kind in range(types):
                 for at in range(5):
                     picked = jnp.zeros((8, width), jnp.float32)
@@ -159,20 +165,14 @@
                         picked = jnp.where(same[second_kind], tables[kind, second_kind][at], picked)
                     table[cell, 3 + 5 * kind + at] = picked
         leading = [cell for cell in some if outside(cell) <= 1]
-        pack = width // 4
-        for start in range(0, len(leading), pack):
-            batch = leading[start : start + pack]
-            turned = jnp.transpose(rows[pl.ds(row_of[batch[0]], width)])
-            for at, (x, y, z) in enumerate(batch):
-                cell = index_of(x, y, z)
-                for axis in range(4):
-                    lane = 4 * at + axis
-                    spread = jnp.broadcast_to(
-                        turned[:, lane : lane + 1], (width, width)
-                    ).reshape((groups, 8, width))
-                    first[cell, axis] = spread
-                for kind in range(1, types):
-                    number_of[cell, kind - 1] = jnp.sum((spread == float(kind)).astype(jnp.float32), 0)
+        for at, cell in enumerate(leading):
+            lines = rows[pl.ds(row_of[cell], 4)]
+            turn[at] = jnp.transpose(jnp.concatenate([lines, lines], 0))
+        for axis in range(4):
+            for at, (x, y, z) in enumerate(leading):
+                first[index_of(x, y, z), axis] = jnp.broadcast_to(
+                    turn[at, :, axis : axis + 1], (width, width)
+                ).reshape((groups, 8, width))
 
     build(inner)
 
@@ -195,62 +195,71 @@
         six = chosen(1) * inverse_6
         coulomb = chosen(2) * inverse
         shift = chosen(3) * (soft_sq * inverse)
-        slope = ((six - twelve) - (coulomb + shift)) * inverse_2
+        drive = (six - twelve) - (coulomb + shift)
+        slope = drive * inverse_2
         forces = (slope * dx, slope * dy, slope * dz)
+        for axis in range(3):
+            force_j[other, axis] -= jnp.sum(forces[axis], 0)
         if ordered is None:
-            for axis in range(3):
-                force_j[other, axis] -= jnp.sum(forces[axis], 0)
-            return forces, (twelve, six, coulomb, shift)
+            terms = (twelve, six, coulomb, shift, slope)
+            return forces, [jnp.sum(term, 0) for term in terms]
         value = twelve * (1.0 / 12.0) - six * (1.0 / 6.0) + coulomb - shift + chosen(4)
-        return forces, jnp.sum(jnp.where(ordered, value, 0.0), 0)
-
-    def role(first_corner, seconds, member, cell_at, energy, depth):
+        pull = drive - soft_core * slope
+        return [jnp.sum(jnp.where(ordered, term, 0.0), 0) for term in (value, pull)]
+
+    def slots(depth):
+        shape = (depth, 8, width)
+        return (
+            lax.broadcasted_iota(jnp.int32, shape, 0) * 8
+            + lax.broadcasted_iota(jnp.int32, shape, 1)
+            - lax.broadcasted_iota(jnp.int32, shape, 2)
+        )
+
+    def load_first(here, span):
+        own_at = tuple(first[here, axis, span] for axis in range(3))
+        kind_at = first[here, 3, span]
+        return own_at, [kind_at == float(kind) for kind in range(1, types)]
+
+    def alone(here, sums, depth):
+        slot_at = slots(depth)
+
+        def step(at, sums):
+            own_at, kinds = load_first(here, pl.ds(at * depth, depth))
+            values = interact(own_at, here, kinds, slot_at + at * (8 * depth) < 0)
+            return tuple(a + b for a, b in zip(sums, values))
+
+        return lax.fori_loop(0, groups // depth, step, sums)
+
+    def role(first_corner, seconds, member, cell_at, sums, depth):
         here = cell_at(first_corner)
         others = [cell_at(which) for which in seconds]
-        part_at = tuple(second_of).index(first_corner) + (1 if seconds[0] else 0)
-        trips = groups // depth
-        slot_at = (
-            lax.broadcasted_iota(jnp.int32, (depth, 8, width), 0) * 8
-            + lax.broadcasted_iota(jnp.int32, (depth, 8, width), 1)
-            - lax.broadcasted_iota(jnp.int32, (depth, 8, width), 2)
-        )
-
-        def step(at, energy):
+        part_at = tuple(second_of).index(first_corner)
+
+        def step(at, sums):
             span = pl.ds(at * depth, depth)
-            own_at = tuple(first[here, axis, span] for axis in range(3))
-            kind_at = first[here, 3, span]
-            kinds = [kind_at == float(kind) for kind in range(1, types)]
+            own_at, kinds = load_first(here, span)
             total = None
-            sums = None
-            for which, other in zip(seconds, others):
-                if which == first_corner:
-                    forces, own_energy = interact(
-                        own_at, other, kinds, slot_at + at * (8 * depth) < 0
-                    )
-                    energy = energy + own_energy
-                else:
-                    forces, terms = interact(own_at, other, kinds)
-                    terms = [jnp.sum(term, 0) for term in terms]
-                    sums = terms if sums is None else [a + b for a, b in zip(sums, terms)]
+            parts = None
+            for other in others:
+                forces, terms = interact(own_at, other, kinds)
+                parts = terms if parts is None else [a + b for a, b in zip(parts, terms)]
                 total = forces if total is None else [a + b for a, b in zip(total, forces)]
-            if sums is not None:
-                energy = energy + (
-                    (sums[0] * (1.0 / 12.0) - sums[1] * (1.0 / 6.0)) + (sums[2] - sums[3])
-                )
+            twelve, six, coulomb, shift, slope = parts
+            value = (twelve * (1.0 / 12.0) - six * (1.0 / 6.0)) + (coulomb - shift)
+            pull = ((six - twelve) - (coulomb + shift)) - soft_core * slope
             for axis in range(3):
                 force_i[part_at, member, axis, span] = total[axis]
-            return energy
-
-        energy = lax.fori_loop(0, trips, step, energy)
-        for which, other in zip(seconds, others):
-            if which != first_corner:
-                numbers = [number_of[here, kind - 1] for kind in range(1, types)]
-                rest = jnp.full((8, width), float(groups))
-                for number in numbers:
-                    rest = rest - number
-                for kind, number in enumerate([rest, *numbers]):
-                    energy = energy + number * table[other, 3 + 5 * kind + 4]
-        return energy
+            return sums[0] + value, sums[1] + pull
+
+        energy, virial = lax.fori_loop(0, groups // depth, step, sums)
+        numbers = [number_of[here, kind - 1] for kind in range(1, types)]
+        rest = jnp.full((8, width), float(groups))
+        for number in numbers:
+            rest = rest - number
+        for other in others:
+            for kind, number in enumerate([rest, *numbers]):
+                energy = energy + number * table[other, 3 + 5 * kind + 4]
+        return energy, virial
 
     def corners(x0, y0, z0):
         def cell_at(which):
@@ -259,21 +268,22 @@
 
         return cell_at
 
-    def one_self(member, energy):
+    def one_self(member, sums):
         z0 = lax.rem(member, sizes[2])
         y0 = lax.rem(member // sizes[2], sizes[1])
         x0 = member // (sizes[2] * sizes[1])
-        return role(0, (0,), member, corners(x0, y0, z0), energy, 4)
-
-    def across(x0, y0, z0, energy):
+        return alone(index_of(x0, y0, z0), sums, 4)
+
+    def across(x0, y0, z0, sums):
         member = (x0 * sizes[1] + y0) * sizes[2] + z0
         cell_at = corners(x0, y0, z0)
         for first_corner, seconds in second_of.items():
             seconds = tuple(which for which in seconds if which)
-            energy = role(first_corner, seconds, member, cell_at, energy, 2 if first_corner == 0 else 4)
-        return energy
-
-    energy = lax.fori_loop(0, members, one_self, jnp.zeros((8, width), jnp.float32))
+            sums = role(first_corner, seconds, member, cell_at, sums, 2 if first_corner == 0 else 4)
+        return sums
+
+    blank = jnp.zeros((8, width), jnp.float32)
+    sums = lax.fori_loop(0, members, one_self, (blank, blank))
 
     pl.semaphore_wait(barrier, greeted)
     halos = []
@@ -296,32 +306,29 @@
 
     less = tuple(size - 1 for size in sizes)
 
-    def inside(at, energy):
+    def inside(at, sums):
         z0 = lax.rem(at, less[2])
         y0 = lax.rem(at // less[2], less[1])
         x0 = at // (less[2] * less[1])
-        return across(x0, y0, z0, energy)
+        return across(x0, y0, z0, sums)
 
     if less[0] * less[1] * less[2]:
-        energy = lax.fori_loop(0, less[0] * less[1] * less[2], inside, energy)
+        sums = lax.fori_loop(0, less[0] * less[1] * less[2], inside, sums)
 
     for copy in halos:
         copy.wait()
     build(outer)
 
-    sheet, bar = sizes[1] * sizes[2], less[0] * sizes[2]
-
-    def border(at, energy):
-        at_sheet, at_bar, at_rest = at, at - sheet, at - sheet - bar
-        on_sheet, on_bar = at < sheet, at < sheet + bar
-        x0 = jnp.where(on_sheet, less[0], jnp.where(on_bar, at_bar // sizes[2], at_rest // max(less[1], 1)))
-        y0 = jnp.where(on_sheet, at_sheet // sizes[2], jnp.where(on_bar, less[1], lax.rem(at_rest, max(less[1], 1))))
-        z0 = jnp.where(on_sheet | on_bar, lax.rem(jnp.where(on_sheet, at_sheet, at_bar), sizes[2]), less[2])
-        return across(x0, y0, z0, energy)
-
-    energy = lax.fori_loop(0, sheet + bar + less[0] * less[1], border, energy)
-
-    virial = jnp.zeros((3, width), jnp.float32)
+    def sheet(at, sums):
+        return across(less[0], at // sizes[2], lax.rem(at, sizes[2]), sums)
+
+    def border(at, sums):
+        on_bar = at < bar
+        rest = at - bar
+        x0 = jnp.where(on_bar, at // sizes[2], rest // max(less[1], 1))
+        y0 = jnp.where(on_bar, less[1], lax.rem(rest, max(less[1], 1)))
+        z0 = jnp.where(on_bar, lax.rem(at, sizes[2]), less[2])
+        return across(x0, y0, z0, sums)
 
     def reduced(cell):
         x, y, z = cell
@@ -331,7 +338,7 @@
         for axis in range(3):
             line = force_j[at_cell, axis]
             partial = None
-            for part_at, first_corner in enumerate((0, 0, 1, 2, 4)):
+            for part_at, first_corner in enumerate(second_of):
                 spot = [at - bit for at, bit in zip(cell, corner_of(first_corner))]
                 if all(0 <= at < size for at, size in zip(spot, sizes)):
                     member = (spot[0] * sizes[1] + spot[1]) * sizes[2] + spot[2]
@@ -344,32 +351,35 @@
             lines.append(jnp.where(held, line, 0.0))
         return jnp.concatenate(lines, 0)
 
-    for cell in outer:
-        force = reduced(cell)
-        react[cell[0], cell[1], cell[2], 0:3] = force
-        virial = virial - force * rows[pl.ds(row_of[cell], 3)]
     backs = []
-    for which in range(1, 8):
-        source = tuple(
-            pl.ds(size, 1) if bit else pl.ds(0, size)
-            for bit, size in zip(corner_of(which), sizes)
-        )
-        copy = pltpu.make_async_remote_copy(
-            src_ref=react.at[source],
-            dst_ref=landed[which - 1],
-            send_sem=back_send.at[which],
-            recv_sem=back_recv.at[which],
-            device_id=neighbour(which, 1),
-            device_id_type=MESH,
-        )
-        copy.start()
-        backs.append(copy)
-    for cell in inner:
-        force = reduced(cell)
-        react[cell[0], cell[1], cell[2], 0:3] = force
-        virial = virial - force * rows[pl.ds(row_of[cell], 3)]
-    part[0:1] = jnp.sum(energy, 0, keepdims=True)
-    part[1:2] = jnp.sum(virial, 0, keepdims=True)
+
+    def give_back(some):
+        for cell in outer:
+            which = sum((at == size) << bit for bit, (at, size) in enumerate(zip(cell, sizes)))
+            if which in some:
+                react[cell[0], cell[1], cell[2], 0:3] = reduced(cell)
+        for which in some:
+            source = tuple(
+                pl.ds(size, 1) if bit else pl.ds(0, size)
+                for bit, size in zip(corner_of(which), sizes)
+            )
+            copy = pltpu.make_async_remote_copy(
+                src_ref=react.at[source],
+                dst_ref=landed[which - 1],
+                send_sem=back_send.at[which],
+                recv_sem=back_recv.at[which],
+                device_id=neighbour(which, 1),
+                device_id_type=MESH,
+            )
+            copy.start()
+            backs.append(copy)
+
+    sums = lax.fori_loop(0, sizes[1] * sizes[2], sheet, sums)
+    give_back((1, 3, 5, 7))
+    bar = less[0] * sizes[2]
+    sums = lax.fori_loop(0, bar + less[0] * less[1], border, sums)
+    part[0:1] = jnp.sum(sums[0], 0, keepdims=True)
+    part[1:2] = jnp.sum(sums[1], 0, keepdims=True)
 
     def send_plane():
         plane_copies = []
@@ -411,6 +421,9 @@
         middle[...] = summed
         plane[at_plane] = summed
         plane_copies = send_plane()
+    give_back((2, 4, 6))
+    for cell in inner:
+        react[cell[0], cell[1], cell[2], 0:3] = reduced(cell)
     for copy in backs:
         copy.wait()
     for x, y, z in inner:
@@ -423,7 +436,8 @@
                     tuple(0 if bit else at for bit, at in zip(bits, spot))
                 ]
         for axis in range(3):
-            forces[axis, x, y, pl.ds(z, 1)] = value[axis : axis + 1]
+            at = ((axis * sizes[0] + x) * sizes[1] + y) * sizes[2] + z
+            forces[pl.ds(at, 1)] = value[axis : axis + 1]
     for copy in plane_copies:
         copy.wait()
     summed = plane[0]
@@ -460,11 +474,11 @@
     ]
     counts = jnp.transpose(counts, (0, 2, 1))
     dma = pltpu.SemaphoreType.DMA
-    return pl.pallas_call(
+    forces, totals = pl.pallas_call(
         functools.partial(step_kernel, normaliser, types),
         name="step",
         out_shape=(
-            jax.ShapeDtypeStruct((3,) + sizes + (width,), f32),
+            jax.ShapeDtypeStruct((3 * members, width), f32),
             jax.ShapeDtypeStruct((2,), f32),
         ),
         in_specs=[smem, smem, smem, hbm, hbm, hbm],
@@ -475,11 +489,12 @@
             pltpu.VMEM(counts.shape, jnp.int32),
             pltpu.VMEM(sizes + (4, width), f32),
             pltpu.VMEM(ext_sizes + (4, width), f32),
-            pltpu.VMEM((4 * cells + width, width), f32),
+            pltpu.VMEM((4 * cells, width), f32),
+            pltpu.VMEM((cells, width, 8), f32),
             pltpu.VMEM((cells, 4, width // 8, 8, width), f32),
             pltpu.VMEM((cells, 3 + 5 * types, 8, width), f32),
             pltpu.VMEM((cells, types - 1, 8, width), f32),
-            pltpu.VMEM((1 + len(second_of), members, 3, width // 8, 8, width), f32),
+            pltpu.VMEM((len(second_of), members, 3, width // 8, 8, width), f32),
             pltpu.VMEM((cells, 3, 8, width), f32),
             pltpu.VMEM(ext_sizes + (4, width), f32),
             pltpu.VMEM((2, width), f32),
@@ -501,6 +516,7 @@
             collective_id=0, has_side_effects=True, vmem_limit_bytes=VMEM_LIMIT
         ),
     )(type_charge, type_sigma, type_epsilon, positions, type_ids, counts)
+    return forces.reshape((3,) + sizes + (width,)), totals
 
 
 def solution(mesh):

time: 45.1 us -> 43.5 us (0.965)
  Pallas kernels: 42.3 us -> 40.7 us
    pallas_call x1, Pallas kernels: 42.3 us -> 40.7 us  [per_device(): pl.pallas_call(functools.partial(step_kernel, normaliser, types), name='s...]
where the time goes in v2:
time: 43.5 us; the launch traced here: 43.2 us
  Pallas kernels  40.7 us (94%)
  local copies, waits for them, and re-layouts  1.86 us (4%)
  between operations  0.65 us (1%)
    pallas_call x1, Pallas kernels, per_device(): pl.pallas_call(functools.partial(step_kernel, normaliser, types), name='s...  40.7 us
    unnamed x4, local copies, waits for them, and re-layouts  1.86 us

profile of v2, /device:TPU:0, one launch (start us, length us, event | category | flops | bytes accessed | tf_op | source)
XLA Modules:
  0.0 43.2 jit_solution(11946953399892463436)
XLA Ops:
  0.6 40.7 %step.1 = (f32[48,128]{1,0:T(8,128)}, f32[2]{0:T(128)}) custom-call(f32[2]{0:T(128)} %charges.1, f32[2]{0:T(128)} %sigmas.1, f32[2]{0:T(128)} %epsilons.1, f32[3,2,4,2,128]{4,3,2,1,0:T(2,128)} %positions.1, s32[2,4,2,128]{3,2,1,0:T(2,128)} %type_ids.1, s32[2,2,4]{2,1,0:T(2,128)} %bitcast.3), custom_call_target="tpu_custom_call" | custom-call | tf_op jit(solution)/shard_map/step/pallas_call | solution.py:477
  41.3 0.0 copy-start
  41.4 1.3 %copy.10 = f32[3,2,4,2,128]{4,3,2,1,0:T(2,128)} copy(f32[3,2,4,2,128]{4,3,2,1,0:T(2,128)} %bitcast.2) | data formatting | bytes 49152
  42.7 0.0 copy-done
  42.7 0.5 %copy.11 = f32[2]{0:T(128)} copy(f32[2]{0:T(128)S(1)} %copy-done) | data formatting | bytes 16
Async XLA Ops:
  41.3 1.4 %copy-start = (f32[2]{0:T(128)S(1)}, f32[2]{0:T(128)}, u32[]{:S(2)}) copy-start(f32[2]{0:T(128)} %get-tuple-element.9) | copy-start | bytes 28

commit v3 on v2

--- a/solution.py
+++ b/solution.py
@@ -14,6 +14,7 @@
 cut_len = cut_sq**0.5
 second_of = {0: (0, 1, 2, 3, 4, 5, 6, 7), 1: (2, 6), 2: (4, 5), 4: (1, 3)}
 direct_limit = 64
+far = 1024.0
 VMEM_LIMIT = 56 * 1024 * 1024
 
 
@@ -28,6 +29,13 @@
             count = lax.axis_size(axis)
             target[axis] = lax.rem(lax.axis_index(axis) + step + count, count)
     return target
+
+
+def split(value):
+    high = value.astype(jnp.bfloat16).astype(jnp.float32)
+    rest = value - high
+    middle = rest.astype(jnp.bfloat16).astype(jnp.float32)
+    return high, middle, rest - middle
 
 
 def type_tables(types, shape, charges, sigmas, epsilons):
@@ -56,7 +64,7 @@
 
 def step_kernel(
     normaliser, types, charges, sigmas, epsilons, positions, type_ids, counts, forces, totals,
-    place_in, kind_in, count_in, own, ext, rows, turn, first, table, number_of, force_i, force_j, react, part,
+    place_in, kind_in, count_in, own, ext, rows, turn, left, right, even, odd, first, table, number_of, force_i, force_j, react, part,
     in_sem, halo_send, halo_recv, back_send, back_recv,
     line, plane, middle, line_send, line_recv, plane_send, plane_recv, *landed,
 ):
@@ -144,6 +152,9 @@
         own[x, y, z] = tile
         ext[x, y, z] = tile
 
+    row = lax.broadcasted_iota(jnp.int32, (8, width), 0)
+    low, top = row % 4, row < 4
+
     def build(some):
         for x, y, z in some:
             cell = index_of(x, y, z)
@@ -152,7 +163,42 @@
             for axis in range(3):
                 table[cell, axis] = jnp.broadcast_to(values[axis : axis + 1], (8, width))
             parked = (row_at == 0) & (values[3:4] < 0.0)
-            rows[pl.ds(row_of[x, y, z], 4)] = jnp.where(parked, x + 4.0, values)
+            lines = jnp.where(parked, x + 4.0, values)
+            rows[pl.ds(row_of[x, y, z], 4)] = lines
+            middle = [0.5 * size for size in ext_sizes]
+            shift = jnp.where(low == 0, middle[0], jnp.where(low == 1, middle[1], middle[2]))
+            both = jnp.concatenate([values, values], 0)
+            live = jnp.broadcast_to(values[3:4], (8, width)) >= 0.0
+            place = jnp.where(live & (low < 3), both - shift, 0.0)
+            norm = jnp.sum((place * place)[0:4], 0, keepdims=True)
+            norm = jnp.where(live, jnp.broadcast_to(norm, (8, width)), far)
+            high, mid, tiny = split(jnp.where(low == 3, norm, place))
+            twice, twice_mid, twice_tiny = split(jnp.where(low == 3, norm + soft_core, -2.0 * place))
+            high_one = jnp.where(row == 3, 1.0, high)
+            twice_one = jnp.where(row == 3, 1.0, twice)
+            right[cell] = jnp.concatenate(
+                [
+                    jnp.where(top, twice_one, jnp.where(row == 7, twice, twice_mid)),
+                    jnp.where(top, twice_one, twice_mid),
+                    jnp.where(top, twice_tiny, jnp.where(row == 7, 1.0, twice)),
+                    jnp.zeros((8, width), jnp.float32),
+                ],
+                0,
+            ).astype(jnp.bfloat16)
+            if outside((x, y, z)) <= 1:
+                turned = jnp.transpose(
+                    jnp.concatenate(
+                        [
+                            jnp.where(row == 7, 1.0, high),
+                            jnp.where(row == 7, 1.0, mid),
+                            jnp.where(top, high_one, tiny),
+                            jnp.concatenate([lines, lines], 0),
+                        ],
+                        0,
+                    )
+                )
+                left[cell] = turned.astype(jnp.bfloat16)
+                turn[cell] = turned
             kind_row = jnp.broadcast_to(values[3:4], (8, width))
             same = [kind_row == float(kind) for kind in range(types)]
             for kind in range(1, types):
@@ -165,18 +211,16 @@
                         picked = jnp.where(same[second_kind], tables[kind, second_kind][at], picked)
                     table[cell, 3 + 5 * kind + at] = picked
         leading = [cell for cell in some if outside(cell) <= 1]
-        for at, cell in enumerate(leading):
-            lines = rows[pl.ds(row_of[cell], 4)]
-            turn[at] = jnp.transpose(jnp.concatenate([lines, lines], 0))
         for axis in range(4):
-            for at, (x, y, z) in enumerate(leading):
-                first[index_of(x, y, z), axis] = jnp.broadcast_to(
-                    turn[at, :, axis : axis + 1], (width, width)
+            for cell in leading:
+                at = index_of(*cell)
+                first[at, axis] = jnp.broadcast_to(
+                    turn[at, :, 24 + axis : 25 + axis], (width, width)
                 ).reshape((groups, 8, width))
 
     build(inner)
 
-    def interact(own_at, other, kinds, ordered=None):
+    def interact(own_at, other, kinds, soft_sq=None, ordered=None):
         xi, yi, zi = own_at
         second = [table[other, at][None] for at in range(per_cell)]
 
@@ -187,7 +231,9 @@
             return value
 
         dx, dy, dz = second[0] - xi, second[1] - yi, second[2] - zi
-        soft_sq = jnp.minimum(dx * dx + dy * dy + dz * dz + soft_core, cut_sq)
+        if soft_sq is None:
+            soft_sq = dx * dx + dy * dy + dz * dz + soft_core
+        soft_sq = jnp.minimum(soft_sq, cut_sq)
         inverse = lax.rsqrt(soft_sq)
         inverse_2 = inverse * inverse
         inverse_6 = inverse_2 * inverse_2 * inverse_2
@@ -225,23 +271,63 @@
 
         def step(at, sums):
             own_at, kinds = load_first(here, pl.ds(at * depth, depth))
-            values = interact(own_at, here, kinds, slot_at + at * (8 * depth) < 0)
+            values = interact(own_at, here, kinds, ordered=slot_at + at * (8 * depth) < 0)
             return tuple(a + b for a, b in zip(sums, values))
 
         return lax.fori_loop(0, groups // depth, step, sums)
 
-    def role(first_corner, seconds, member, cell_at, sums, depth):
+    def levels(energy, here, others):
+        numbers = [number_of[here, kind - 1] for kind in range(1, types)]
+        rest = jnp.full((8, width), float(groups))
+        for number in numbers:
+            rest = rest - number
+        for other in others:
+            for kind, number in enumerate([rest, *numbers]):
+                energy = energy + number * table[other, 3 + 5 * kind + 4]
+        return energy
+
+    roles = {
+        first_corner: tuple(which for which in seconds if which)
+        for first_corner, seconds in second_of.items()
+    }
+    depth = 4
+    trips = groups // depth
+    offset_of = {}
+    for first_corner, seconds in roles.items():
+        offset_of[first_corner] = sum(len(roles[corner]) for corner in offset_of)
+
+    def distances(store, cell_at, chunk, first_corner):
+        wide = 8 * depth
+        lefts = left[cell_at(first_corner), pl.ds(chunk * wide, wide)]
+        seconds = roles[first_corner]
+        for at in range(0, len(seconds), 2):
+            some = [right[cell_at(which)] for which in seconds[at : at + 2]]
+            found = jnp.dot(
+                lefts,
+                jnp.concatenate(some, 1) if len(some) > 1 else some[0],
+                preferred_element_type=jnp.float32,
+            )
+            for n in range(len(some)):
+                store[offset_of[first_corner] + at + n, pl.ds(chunk * depth, depth)] = found[:, n * width : (n + 1) * width].reshape(
+                    (depth, 8, width)
+                )
+
+    def role(first_corner, member, cell_at, chunk, held, sums):
         here = cell_at(first_corner)
-        others = [cell_at(which) for which in seconds]
         part_at = tuple(second_of).index(first_corner)
-
-        def step(at, sums):
-            span = pl.ds(at * depth, depth)
+        fine = 4 if first_corner == 0 else 4
+        for start in range(0, depth, fine):
+            span = pl.ds(chunk * depth + start, fine)
             own_at, kinds = load_first(here, span)
             total = None
             parts = None
-            for other in others:
-                forces, terms = interact(own_at, other, kinds)
+            for n, which in enumerate(roles[first_corner]):
+                forces, terms = interact(
+                    own_at,
+                    cell_at(which),
+                    kinds,
+                    held[offset_of[first_corner] + n, pl.ds(chunk * depth + start, fine)],
+                )
                 parts = terms if parts is None else [a + b for a, b in zip(parts, terms)]
                 total = forces if total is None else [a + b for a, b in zip(total, forces)]
             twelve, six, coulomb, shift, slope = parts
@@ -249,17 +335,8 @@
             pull = ((six - twelve) - (coulomb + shift)) - soft_core * slope
             for axis in range(3):
                 force_i[part_at, member, axis, span] = total[axis]
-            return sums[0] + value, sums[1] + pull
-
-        energy, virial = lax.fori_loop(0, groups // depth, step, sums)
-        numbers = [number_of[here, kind - 1] for kind in range(1, types)]
-        rest = jnp.full((8, width), float(groups))
-        for number in numbers:
-            rest = rest - number
-        for other in others:
-            for kind, number in enumerate([rest, *numbers]):
-                energy = energy + number * table[other, 3 + 5 * kind + 4]
-        return energy, virial
+            sums = sums[0] + value, sums[1] + pull
+        return sums
 
     def corners(x0, y0, z0):
         def cell_at(which):
@@ -274,16 +351,41 @@
         x0 = member // (sizes[2] * sizes[1])
         return alone(index_of(x0, y0, z0), sums, 4)
 
-    def across(x0, y0, z0, sums):
-        member = (x0 * sizes[1] + y0) * sizes[2] + z0
-        cell_at = corners(x0, y0, z0)
-        for first_corner, seconds in second_of.items():
-            seconds = tuple(which for which in seconds if which)
-            sums = role(first_corner, seconds, member, cell_at, sums, 2 if first_corner == 0 else 4)
+    def across(homes, sums):
+        stores = (even, odd)
+        for first_corner in roles:
+            for chunk in range(trips):
+                distances(even, corners(*homes[0]), chunk, first_corner)
+        for at, (x0, y0, z0) in enumerate(homes):
+            member = (x0 * sizes[1] + y0) * sizes[2] + z0
+            cell_at = corners(x0, y0, z0)
+            held, store = stores[at % 2], stores[(at + 1) % 2]
+            after = corners(*homes[at + 1]) if at + 1 < len(homes) else None
+
+            def step(chunk, sums, some):
+                for first_corner in some:
+                    if after is not None:
+                        distances(store, after, chunk, first_corner)
+                for first_corner in some:
+                    sums = role(first_corner, member, cell_at, chunk, held, sums)
+                return sums
+
+            for some in ((0,), tuple(corner for corner in roles if corner)):
+                sums = lax.fori_loop(0, trips, functools.partial(step, some=some), sums)
         return sums
 
     blank = jnp.zeros((8, width), jnp.float32)
     sums = lax.fori_loop(0, members, one_self, (blank, blank))
+
+    def base_level(member, energy):
+        z0 = lax.rem(member, sizes[2])
+        y0 = lax.rem(member // sizes[2], sizes[1])
+        x0 = member // (sizes[2] * sizes[1])
+        cell_at = corners(x0, y0, z0)
+        for first_corner, seconds in roles.items():
+            energy = levels(energy, cell_at(first_corner), [cell_at(which) for which in seconds])
+        return energy
+
 
     pl.semaphore_wait(barrier, greeted)
     halos = []
@@ -306,29 +408,18 @@
 
     less = tuple(size - 1 for size in sizes)
 
-    def inside(at, sums):
-        z0 = lax.rem(at, less[2])
-        y0 = lax.rem(at // less[2], less[1])
-        x0 = at // (less[2] * less[1])
-        return across(x0, y0, z0, sums)
-
-    if less[0] * less[1] * less[2]:
-        sums = lax.fori_loop(0, less[0] * less[1] * less[2], inside, sums)
+    homes = [
+        (x, y, z) for x in range(sizes[0]) for y in range(sizes[1]) for z in range(sizes[2])
+    ]
+    inside = [home for home in homes if all(at < most for at, most in zip(home, less))]
+    sheet = [home for home in homes if home[0] == less[0]]
+    border = [home for home in homes if home not in inside and home not in sheet]
+    if inside:
+        sums = across(inside, sums)
 
     for copy in halos:
         copy.wait()
     build(outer)
-
-    def sheet(at, sums):
-        return across(less[0], at // sizes[2], lax.rem(at, sizes[2]), sums)
-
-    def border(at, sums):
-        on_bar = at < bar
-        rest = at - bar
-        x0 = jnp.where(on_bar, at // sizes[2], rest // max(less[1], 1))
-        y0 = jnp.where(on_bar, less[1], lax.rem(rest, max(less[1], 1)))
-        z0 = jnp.where(on_bar, lax.rem(at, sizes[2]), less[2])
-        return across(x0, y0, z0, sums)
 
     def reduced(cell):
         x, y, z = cell
@@ -374,10 +465,12 @@
             copy.start()
             backs.append(copy)
 
-    sums = lax.fori_loop(0, sizes[1] * sizes[2], sheet, sums)
+    sums = across(sheet, sums)
     give_back((1, 3, 5, 7))
-    bar = less[0] * sizes[2]
-    sums = lax.fori_loop(0, bar + less[0] * less[1], border, sums)
+    energy = lax.fori_loop(0, members, base_level, sums[0])
+    sums = energy, sums[1]
+    if border:
+        sums = across(border, sums)
     part[0:1] = jnp.sum(sums[0], 0, keepdims=True)
     part[1:2] = jnp.sum(sums[1], 0, keepdims=True)
 
@@ -490,7 +583,11 @@
             pltpu.VMEM(sizes + (4, width), f32),
             pltpu.VMEM(ext_sizes + (4, width), f32),
             pltpu.VMEM((4 * cells, width), f32),
-            pltpu.VMEM((cells, width, 8), f32),
+            pltpu.VMEM((cells, width, 32), f32),
+            pltpu.VMEM((cells, width, 32), jnp.bfloat16),
+            pltpu.VMEM((cells, 32, width), jnp.bfloat16),
+            pltpu.VMEM((13, width // 8, 8, width), f32),
+            pltpu.VMEM((13, width // 8, 8, width), f32),
             pltpu.VMEM((cells, 4, width // 8, 8, width), f32),
             pltpu.VMEM((cells, 3 + 5 * types, 8, width), f32),
             pltpu.VMEM((cells, types - 1, 8, width), f32),

time: 43.5 us -> 41.6 us (0.956)
  Pallas kernels: 40.7 us -> 38.9 us
    pallas_call x1, Pallas kernels: 40.7 us -> 38.9 us  [per_device(): pl.pallas_call(functools.partial(step_kernel, normaliser, types), name='s...]
where the time goes in v3:
time: 41.6 us; the launch traced here: 41.4 us
  Pallas kernels  38.9 us (94%)
  local copies, waits for them, and re-layouts  1.86 us (4%)
  between operations  0.65 us (2%)
    pallas_call x1, Pallas kernels, per_device(): pl.pallas_call(functools.partial(step_kernel, normaliser, types), name='s...  38.9 us
    unnamed x4, local copies, waits for them, and re-layouts  1.86 us

profile of v3, /device:TPU:0, one launch (start us, length us, event | category | flops | bytes accessed | tf_op | source)
XLA Modules:
  0.0 41.4 jit_solution(7348459868237830396)
XLA Ops:
  0.6 38.9 %step.1 = (f32[48,128]{1,0:T(8,128)}, f32[2]{0:T(128)}) custom-call(f32[2]{0:T(128)} %charges.1, f32[2]{0:T(128)} %sigmas.1, f32[2]{0:T(128)} %epsilons.1, f32[3,2,4,2,128]{4,3,2,1,0:T(2,128)} %positions.1, s32[2,4,2,128]{3,2,1,0:T(2,128)} %type_ids.1, s32[2,2,4]{2,1,0:T(2,128)} %bitcast.3), custom_call_target="tpu_custom_call" | custom-call | tf_op jit(solution)/shard_map/step/pallas_call | solution.py:570
  39.5 0.0 copy-start
  39.5 1.3 %copy.10 = f32[3,2,4,2,128]{4,3,2,1,0:T(2,128)} copy(f32[3,2,4,2,128]{4,3,2,1,0:T(2,128)} %bitcast.2) | data formatting | bytes 49152
  40.9 0.0 copy-done
  40.9 0.5 %copy.11 = f32[2]{0:T(128)} copy(f32[2]{0:T(128)S(1)} %copy-done) | data formatting | bytes 16
Async XLA Ops:
  39.5 1.4 %copy-start = (f32[2]{0:T(128)S(1)}, f32[2]{0:T(128)}, u32[]{:S(2)}) copy-start(f32[2]{0:T(128)} %get-tuple-element.9) | copy-start | bytes 28

commit v4 on v3

--- a/solution.py
+++ b/solution.py
@@ -15,7 +15,7 @@
 second_of = {0: (0, 1, 2, 3, 4, 5, 6, 7), 1: (2, 6), 2: (4, 5), 4: (1, 3)}
 direct_limit = 64
 far = 1024.0
-VMEM_LIMIT = 56 * 1024 * 1024
+VMEM_LIMIT = 40 * 1024 * 1024
 
 
 def corner_of(which):
@@ -64,7 +64,7 @@
 
 def step_kernel(
     normaliser, types, charges, sigmas, epsilons, positions, type_ids, counts, forces, totals,
-    place_in, kind_in, count_in, own, ext, rows, turn, left, right, even, odd, first, table, number_of, force_i, force_j, react, part,
+    place_in, kind_in, count_in, own, ext, rows, pick, left, right, even, odd, first, table, number_of, force_i, force_j, react, part,
     in_sem, halo_send, halo_recv, back_send, back_recv,
     line, plane, middle, line_send, line_recv, plane_send, plane_recv, *landed,
 ):
@@ -131,14 +131,13 @@
         return (x * ext_sizes[1] + y) * ext_sizes[2] + z
 
     ordered = sorted(cells, key=outside)
-    row_of = {cell: 4 * at for at, cell in enumerate(ordered)}
+    row_of = {cell: at for at, cell in enumerate(ordered)}
     inner = [cell for cell in ordered if outside(cell) == 0]
     outer = [cell for cell in ordered if outside(cell) > 0]
 
     tables = type_tables(types, (8, width), charges, sigmas, epsilons)
     force_j[...] = jnp.zeros(force_j.shape, jnp.float32)
     react[...] = jnp.zeros(react.shape, jnp.float32)
-    row_at = lax.broadcasted_iota(jnp.int32, (4, width), 0)
     slot = lax.broadcasted_iota(jnp.int32, (1, width), 1)
 
     for load in loads:
@@ -154,22 +153,25 @@
 
     row = lax.broadcasted_iota(jnp.int32, (8, width), 0)
     low, top = row % 4, row < 4
+    center = [0.5 * size for size in ext_sizes]
+    wide_row = lax.broadcasted_iota(jnp.int32, (32, 4 * width), 0)
+    wide_axis = lax.broadcasted_iota(jnp.int32, (32, 4 * width), 1) // width
+    picked = (wide_row == wide_axis) | (wide_row == wide_axis + 8) | (wide_row == wide_axis + 20)
+    picked = jnp.where(picked & (wide_axis < 3), 1.0, 0.0)
+    picked = jnp.where((wide_axis == 3) & (wide_row == 27), 1.0, picked)
+    pick[...] = picked.astype(jnp.bfloat16)
 
     def build(some):
         for x, y, z in some:
             cell = index_of(x, y, z)
-            base = jnp.where(row_at == 0, x, jnp.where(row_at == 1, y, jnp.where(row_at == 2, z, 0)))
-            values = ext[x, y, z] + base.astype(jnp.float32)
+            base = jnp.where(low == 0, x - center[0], jnp.where(low == 1, y - center[1], z - center[2]))
+            lines = ext[x, y, z]
+            rows[pl.ds(row_of[x, y, z], 1)] = lines[3:4]
+            both = jnp.concatenate([lines, lines], 0)
+            live = jnp.broadcast_to(lines[3:4], (8, width)) >= 0.0
+            place = jnp.where(live & (low < 3), both + base, 0.0)
             for axis in range(3):
-                table[cell, axis] = jnp.broadcast_to(values[axis : axis + 1], (8, width))
-            parked = (row_at == 0) & (values[3:4] < 0.0)
-            lines = jnp.where(parked, x + 4.0, values)
-            rows[pl.ds(row_of[x, y, z], 4)] = lines
-            middle = [0.5 * size for size in ext_sizes]
-            shift = jnp.where(low == 0, middle[0], jnp.where(low == 1, middle[1], middle[2]))
-            both = jnp.concatenate([values, values], 0)
-            live = jnp.broadcast_to(values[3:4], (8, width)) >= 0.0
-            place = jnp.where(live & (low < 3), both - shift, 0.0)
+                table[cell, axis] = jnp.broadcast_to(place[axis : axis + 1], (8, width))
             norm = jnp.sum((place * place)[0:4], 0, keepdims=True)
             norm = jnp.where(live, jnp.broadcast_to(norm, (8, width)), far)
             high, mid, tiny = split(jnp.where(low == 3, norm, place))
@@ -192,14 +194,19 @@
                             jnp.where(row == 7, 1.0, high),
                             jnp.where(row == 7, 1.0, mid),
                             jnp.where(top, high_one, tiny),
-                            jnp.concatenate([lines, lines], 0),
+                            both,
                         ],
                         0,
                     )
                 )
-                left[cell] = turned.astype(jnp.bfloat16)
-                turn[cell] = turned
-            kind_row = jnp.broadcast_to(values[3:4], (8, width))
+                turned = turned.astype(jnp.bfloat16)
+                left[cell] = turned
+                spread = jnp.dot(turned, pick[...], preferred_element_type=jnp.float32)
+                for axis in range(4):
+                    first[cell, axis] = spread[:, axis * width : (axis + 1) * width].reshape(
+                        (groups, 8, width)
+                    )
+            kind_row = jnp.broadcast_to(lines[3:4], (8, width))
             same = [kind_row == float(kind) for kind in range(types)]
             for kind in range(1, types):
                 total = jnp.sum(same[kind].astype(jnp.float32), 1, keepdims=True) * 0.125
@@ -210,17 +217,10 @@
                     for second_kind in range(types):
                         picked = jnp.where(same[second_kind], tables[kind, second_kind][at], picked)
                     table[cell, 3 + 5 * kind + at] = picked
-        leading = [cell for cell in some if outside(cell) <= 1]
-        for axis in range(4):
-            for cell in leading:
-                at = index_of(*cell)
-                first[at, axis] = jnp.broadcast_to(
-                    turn[at, :, 24 + axis : 25 + axis], (width, width)
-                ).reshape((groups, 8, width))
 
     build(inner)
 
-    def interact(own_at, other, kinds, soft_sq=None, ordered=None):
+    def interact(own_at, other, kinds, soft_sq, ordered=None):
         xi, yi, zi = own_at
         second = [table[other, at][None] for at in range(per_cell)]
 
@@ -231,8 +231,6 @@
             return value
 
         dx, dy, dz = second[0] - xi, second[1] - yi, second[2] - zi
-        if soft_sq is None:
-            soft_sq = dx * dx + dy * dy + dz * dz + soft_core
         soft_sq = jnp.minimum(soft_sq, cut_sq)
         inverse = lax.rsqrt(soft_sq)
         inverse_2 = inverse * inverse
@@ -266,15 +264,20 @@
         kind_at = first[here, 3, span]
         return own_at, [kind_at == float(kind) for kind in range(1, types)]
 
-    def alone(here, sums, depth):
-        slot_at = slots(depth)
-
-        def step(at, sums):
-            own_at, kinds = load_first(here, pl.ds(at * depth, depth))
-            values = interact(own_at, here, kinds, ordered=slot_at + at * (8 * depth) < 0)
-            return tuple(a + b for a, b in zip(sums, values))
-
-        return lax.fori_loop(0, groups // depth, step, sums)
+    def alone(here, held, sums):
+        slot_at = slots(4)
+        for start in range(0, groups, 4):
+            span = pl.ds(start, 4)
+            own_at, kinds = load_first(here, span)
+            values = interact(
+                own_at, here, kinds, held[0, span], ordered=slot_at + start * 8 < 0
+            )
+            sums = tuple(a + b for a, b in zip(sums, values))
+        return sums
+
+    def apart(store, here):
+        found = jnp.dot(left[here], right[here], preferred_element_type=jnp.float32)
+        store[0] = found.reshape((groups, 8, width))
 
     def levels(energy, here, others):
         numbers = [number_of[here, kind - 1] for kind in range(1, types)]
@@ -345,11 +348,19 @@
 
         return cell_at
 
-    def one_self(member, sums):
-        z0 = lax.rem(member, sizes[2])
-        y0 = lax.rem(member // sizes[2], sizes[1])
-        x0 = member // (sizes[2] * sizes[1])
-        return alone(index_of(x0, y0, z0), sums, 4)
+    def one_pair(at, sums):
+        cell = [
+            index_of(
+                member // (sizes[2] * sizes[1]),
+                lax.rem(member // sizes[2], sizes[1]),
+                lax.rem(member, sizes[2]),
+            )
+            for member in (2 * at, 2 * at + 1, jnp.minimum(2 * at + 2, members - 1))
+        ]
+        apart(odd, cell[1])
+        sums = alone(cell[0], even, sums)
+        apart(even, cell[2])
+        return alone(cell[1], odd, sums)
 
     def across(homes, sums):
         stores = (even, odd)
@@ -375,7 +386,8 @@
         return sums
 
     blank = jnp.zeros((8, width), jnp.float32)
-    sums = lax.fori_loop(0, members, one_self, (blank, blank))
+    apart(even, index_of(0, 0, 0))
+    sums = lax.fori_loop(0, members // 2, one_pair, (blank, blank))
 
     def base_level(member, energy):
         z0 = lax.rem(member, sizes[2])
@@ -424,7 +436,7 @@
     def reduced(cell):
         x, y, z = cell
         at_cell = index_of(x, y, z)
-        held = rows[pl.ds(row_of[cell] + 3, 1)] >= 0.0
+        held = rows[pl.ds(row_of[cell], 1)] >= 0.0
         lines = []
         for axis in range(3):
             line = force_j[at_cell, axis]
@@ -566,6 +578,13 @@
         for which in range(1, 8)
     ]
     counts = jnp.transpose(counts, (0, 2, 1))
+    positions, type_ids, counts = (
+        pltpu.with_memory_space_constraint(value, pltpu.HBM) for value in (positions, type_ids, counts)
+    )
+    type_charge, type_sigma, type_epsilon = (
+        pltpu.with_memory_space_constraint(value, pltpu.HBM)
+        for value in (type_charge, type_sigma, type_epsilon)
+    )
     dma = pltpu.SemaphoreType.DMA
     forces, totals = pl.pallas_call(
         functools.partial(step_kernel, normaliser, types),
@@ -582,8 +601,8 @@
             pltpu.VMEM(counts.shape, jnp.int32),
             pltpu.VMEM(sizes + (4, width), f32),
             pltpu.VMEM(ext_sizes + (4, width), f32),
-            pltpu.VMEM((4 * cells, width), f32),
-            pltpu.VMEM((cells, width, 32), f32),
+            pltpu.VMEM((cells, width), f32),
+            pltpu.VMEM((32, 4 * width), jnp.bfloat16),
             pltpu.VMEM((cells, width, 32), jnp.bfloat16),
             pltpu.VMEM((cells, 32, width), jnp.bfloat16),
             pltpu.VMEM((13, width // 8, 8, width), f32),

time: 41.6 us -> 39.6 us (0.952)
  Pallas kernels: 38.9 us -> 37.6 us
  local copies, waits for them, and re-layouts: 1.86 us -> 1.12 us
    pallas_call x1, Pallas kernels: 38.9 us -> 37.6 us  [per_device(): pl.pallas_call(functools.partial(step_kernel, normaliser, types), name='s...]
    unnamed x4 -> x2, local copies, waits for them, and re-layouts: 1.86 us -> 1.12 us
where the time goes in v4:
time: 39.6 us; the launch traced here: 39.4 us
  Pallas kernels  37.6 us (95%)
  local copies, waits for them, and re-layouts  1.12 us (3%)
  between operations  0.64 us (2%)
    pallas_call x1, Pallas kernels, per_device(): pl.pallas_call(functools.partial(step_kernel, normaliser, types), name='s...  37.6 us
    unnamed x2, local copies, waits for them, and re-layouts  1.12 us

profile of v4, /device:TPU:0, one launch (start us, length us, event | category | flops | bytes accessed | tf_op | source)
XLA Modules:
  0.0 39.4 jit_solution(1635231682798325227)
XLA Ops:
  0.6 37.6 %step.1 = (f32[48,128]{1,0:T(8,128)S(1)}, f32[2]{0:T(128)S(1)}) custom-call(f32[2]{0:T(128)} %charges.1, f32[2]{0:T(128)} %sigmas.1, f32[2]{0:T(128)} %epsilons.1, f32[3,2,4,2,128]{4,3,2,1,0:T(2,128)} %positions.1, s32[2,4,2,128]{3,2,1,0:T(2,128)} %type_ids.1, s32[2,2,4]{2,1,0:T(2,128)} %bitcast.3), custom_call_target="tpu_custom_call" | custom-call | tf_op jit(solution)/shard_map/step/pallas_call | solution.py:589
  38.3 0.6 %copy.10 = f32[3,2,4,2,128]{4,3,2,1,0:T(2,128)} copy(f32[3,2,4,2,128]{4,3,2,1,0:T(2,128)S(1)} %bitcast.2) | data formatting | bytes 49152
  38.9 0.5 %copy.11 = f32[2]{0:T(128)} copy(f32[2]{0:T(128)S(1)} %get-tuple-element.9) | data formatting | bytes 16

commit v5 on v4

--- a/solution.py
+++ b/solution.py
@@ -362,27 +362,38 @@
         apart(even, cell[2])
         return alone(cell[1], odd, sums)
 
-    def across(homes, sums):
-        stores = (even, odd)
-        for first_corner in roles:
-            for chunk in range(trips):
-                distances(even, corners(*homes[0]), chunk, first_corner)
-        for at, (x0, y0, z0) in enumerate(homes):
+    def across(count, locate, sums):
+        def one_home(home, after, held, store, sums):
+            x0, y0, z0 = home
             member = (x0 * sizes[1] + y0) * sizes[2] + z0
             cell_at = corners(x0, y0, z0)
-            held, store = stores[at % 2], stores[(at + 1) % 2]
-            after = corners(*homes[at + 1]) if at + 1 < len(homes) else None
+            after_at = None if after is None else corners(*after)
 
             def step(chunk, sums, some):
                 for first_corner in some:
                     if after is not None:
-                        distances(store, after, chunk, first_corner)
+                        distances(store, after_at, chunk, first_corner)
                 for first_corner in some:
                     sums = role(first_corner, member, cell_at, chunk, held, sums)
                 return sums
 
             for some in ((0,), tuple(corner for corner in roles if corner)):
                 sums = lax.fori_loop(0, trips, functools.partial(step, some=some), sums)
+            return sums
+
+        def two_homes(at, sums):
+            spot = 2 * at
+            sums = one_home(locate(spot), locate(spot + 1), even, odd, sums)
+            after = locate(jnp.minimum(spot + 2, count - 1))
+            return one_home(locate(spot + 1), after, odd, even, sums)
+
+        cell_at = corners(*locate(0))
+        for first_corner in roles:
+            for chunk in range(trips):
+                distances(even, cell_at, chunk, first_corner)
+        sums = lax.fori_loop(0, count // 2, two_homes, sums)
+        if count % 2:
+            sums = one_home(locate(count - 1), None, even, odd, sums)
         return sums
 
     blank = jnp.zeros((8, width), jnp.float32)
@@ -420,14 +431,23 @@
 
     less = tuple(size - 1 for size in sizes)
 
-    homes = [
-        (x, y, z) for x in range(sizes[0]) for y in range(sizes[1]) for z in range(sizes[2])
-    ]
-    inside = [home for home in homes if all(at < most for at, most in zip(home, less))]
-    sheet = [home for home in homes if home[0] == less[0]]
-    border = [home for home in homes if home not in inside and home not in sheet]
-    if inside:
-        sums = across(inside, sums)
+    def inside(at):
+        return at // (less[2] * less[1]), lax.rem(at // less[2], less[1]), lax.rem(at, less[2])
+
+    def sheet(at):
+        return less[0], at // sizes[2], lax.rem(at, sizes[2])
+
+    def border(at):
+        on_bar = at < bar
+        rest = at - bar
+        x0 = jnp.where(on_bar, at // sizes[2], rest // max(less[1], 1))
+        y0 = jnp.where(on_bar, less[1], lax.rem(rest, max(less[1], 1)))
+        z0 = jnp.where(on_bar, lax.rem(at, sizes[2]), less[2])
+        return x0, y0, z0
+
+    bar = less[0] * sizes[2]
+    if less[0] * less[1] * less[2]:
+        sums = across(less[0] * less[1] * less[2], inside, sums)
 
     for copy in halos:
         copy.wait()
@@ -477,12 +497,12 @@
             copy.start()
             backs.append(copy)
 
-    sums = across(sheet, sums)
+    sums = across(sizes[1] * sizes[2], sheet, sums)
     give_back((1, 3, 5, 7))
     energy = lax.fori_loop(0, members, base_level, sums[0])
     sums = energy, sums[1]
-    if border:
-        sums = across(border, sums)
+    if less[0]:
+        sums = across(bar + less[0] * less[1], border, sums)
     part[0:1] = jnp.sum(sums[0], 0, keepdims=True)
     part[1:2] = jnp.sum(sums[1], 0, keepdims=True)
 

time: 39.6 us -> 40.4 us (1.020)
  Pallas kernels: 37.6 us -> 38.4 us
    pallas_call x1, Pallas kernels: 37.6 us -> 38.4 us  [per_device(): pl.pallas_call(functools.partial(step_kernel, normaliser, types), name='s...]
where the time goes in v5:
time: 40.4 us; the launch traced here: 40.2 us
  Pallas kernels  38.4 us (95%)
  local copies, waits for them, and re-layouts  1.12 us (3%)
  between operations  0.64 us (2%)
    pallas_call x1, Pallas kernels, per_device(): pl.pallas_call(functools.partial(step_kernel, normaliser, types), name='s...  38.4 us
    unnamed x2, local copies, waits for them, and re-layouts  1.12 us

profile of v5, /device:TPU:0, one launch (start us, length us, event | category | flops | bytes accessed | tf_op | source)
XLA Modules:
  0.0 40.2 jit_solution(12116753540548732533)
XLA Ops:
  0.6 38.4 %step.1 = (f32[48,128]{1,0:T(8,128)S(1)}, f32[2]{0:T(128)S(1)}) custom-call(f32[2]{0:T(128)} %charges.1, f32[2]{0:T(128)} %sigmas.1, f32[2]{0:T(128)} %epsilons.1, f32[3,2,4,2,128]{4,3,2,1,0:T(2,128)} %positions.1, s32[2,4,2,128]{3,2,1,0:T(2,128)} %type_ids.1, s32[2,2,4]{2,1,0:T(2,128)} %bitcast.3), custom_call_target="tpu_custom_call" | custom-call | tf_op jit(solution)/shard_map/step/pallas_call | solution.py:609
  39.1 0.6 %copy.10 = f32[3,2,4,2,128]{4,3,2,1,0:T(2,128)} copy(f32[3,2,4,2,128]{4,3,2,1,0:T(2,128)S(1)} %bitcast.2) | data formatting | bytes 49152
  39.7 0.5 %copy.11 = f32[2]{0:T(128)} copy(f32[2]{0:T(128)S(1)} %get-tuple-element.9) | data formatting | bytes 16

commit v6 on v4

--- a/solution.py
+++ b/solution.py
@@ -63,8 +63,8 @@
 
 
 def step_kernel(
-    normaliser, types, charges, sigmas, epsilons, positions, type_ids, counts, forces, totals,
-    place_in, kind_in, count_in, own, ext, rows, pick, left, right, even, odd, first, table, number_of, force_i, force_j, react, part,
+    normaliser, types, charge_all, sigma_all, epsilon_all, positions, type_ids, counts,
+    forces, totals, charges, sigmas, epsilons, place_in, kind_in, count_in, own, ext, rows, pick, left, right, even, odd, first, table, number_of, force_i, force_j, react, part,
     in_sem, halo_send, halo_recv, back_send, back_recv,
     line, plane, middle, line_send, line_recv, plane_send, plane_recv, *landed,
 ):
@@ -82,7 +82,14 @@
     loads = [
         pltpu.make_async_copy(source, target, in_sem.at[at])
         for at, (source, target) in enumerate(
-            ((positions, place_in), (type_ids, kind_in), (counts, count_in))
+            (
+                (positions, place_in),
+                (type_ids, kind_in),
+                (counts, count_in),
+                (charge_all, charges),
+                (sigma_all, sigmas),
+                (epsilon_all, epsilons),
+            )
         )
     ]
     for load in loads:
@@ -135,13 +142,13 @@
     inner = [cell for cell in ordered if outside(cell) == 0]
     outer = [cell for cell in ordered if outside(cell) > 0]
 
-    tables = type_tables(types, (8, width), charges, sigmas, epsilons)
     force_j[...] = jnp.zeros(force_j.shape, jnp.float32)
     react[...] = jnp.zeros(react.shape, jnp.float32)
     slot = lax.broadcasted_iota(jnp.int32, (1, width), 1)
 
     for load in loads:
         load.wait()
+    tables = type_tables(types, (8, width), charges, sigmas, epsilons)
     for x, y, z in inner:
         lines = [place_in[axis, x, y, pl.ds(z, 1)] for axis in range(3)]
         kind = kind_in[x, y, pl.ds(z, 1)].astype(jnp.float32)
@@ -381,7 +388,7 @@
                     sums = role(first_corner, member, cell_at, chunk, held, sums)
                 return sums
 
-            for some in ((0,), tuple(corner for corner in roles if corner)):
+            for some in (tuple(roles),):
                 sums = lax.fori_loop(0, trips, functools.partial(step, some=some), sums)
         return sums
 
@@ -593,9 +600,12 @@
             jax.ShapeDtypeStruct((3 * members, width), f32),
             jax.ShapeDtypeStruct((2,), f32),
         ),
-        in_specs=[smem, smem, smem, hbm, hbm, hbm],
+        in_specs=[hbm] * 6,
         out_specs=(vmem, smem),
         scratch_shapes=[
+            pltpu.SMEM((types,), f32),
+            pltpu.SMEM((types,), f32),
+            pltpu.SMEM((types,), f32),
             pltpu.VMEM(positions.shape, f32),
             pltpu.VMEM(type_ids.shape, jnp.int32),
             pltpu.VMEM(counts.shape, jnp.int32),
@@ -614,7 +624,7 @@
             pltpu.VMEM((cells, 3, 8, width), f32),
             pltpu.VMEM(ext_sizes + (4, width), f32),
             pltpu.VMEM((2, width), f32),
-            dma((3,)),
+            dma((6,)),
             dma((8,)),
             dma((8,)),
             dma((8,)),

time: 39.6 us -> 37.8 us (0.955)
  Pallas kernels: 37.6 us -> 35.9 us
    pallas_call x1, Pallas kernels: 37.6 us -> 35.9 us  [per_device(): pl.pallas_call(functools.partial(step_kernel, normaliser, types), name='s...]
where the time goes in v6:
time: 37.8 us; the launch traced here: 37.7 us
  Pallas kernels  35.9 us (95%)
  local copies, waits for them, and re-layouts  1.12 us (3%)
  between operations  0.64 us (2%)
    pallas_call x1, Pallas kernels, per_device(): pl.pallas_call(functools.partial(step_kernel, normaliser, types), name='s...  35.9 us
    unnamed x2, local copies, waits for them, and re-layouts  1.12 us

profile of v6, /device:TPU:0, one launch (start us, length us, event | category | flops | bytes accessed | tf_op | source)
XLA Modules:
  0.0 37.7 jit_solution(15207706412321227337)
XLA Ops:
  0.6 35.9 %step.1 = (f32[48,128]{1,0:T(8,128)S(1)}, f32[2]{0:T(128)S(1)}) custom-call(f32[2]{0:T(128)} %charge_all.1, f32[2]{0:T(128)} %sigma_all.1, f32[2]{0:T(128)} %epsilon_all.1, f32[3,2,4,2,128]{4,3,2,1,0:T(2,128)} %positions.1, s32[2,4,2,128]{3,2,1,0:T(2,128)} %type_ids.1, s32[2,2,4]{2,1,0:T(2,128)} %bitcast.3), custom_call_target="tpu_custom_call" | custom-call | tf_op jit(solution)/shard_map/step/pallas_call | solution.py:596
  36.5 0.6 %copy.10 = f32[3,2,4,2,128]{4,3,2,1,0:T(2,128)} copy(f32[3,2,4,2,128]{4,3,2,1,0:T(2,128)S(1)} %bitcast.2) | data formatting | bytes 49152
  37.1 0.5 %copy.11 = f32[2]{0:T(128)} copy(f32[2]{0:T(128)S(1)} %get-tuple-element.9) | data formatting | bytes 16

commit v7 on v6

--- a/solution.py
+++ b/solution.py
@@ -369,12 +369,14 @@
         apart(even, cell[2])
         return alone(cell[1], odd, sums)
 
-    def across(homes, sums):
+    def across(homes, sums, pause=None, then=None):
         stores = (even, odd)
         for first_corner in roles:
             for chunk in range(trips):
                 distances(even, corners(*homes[0]), chunk, first_corner)
         for at, (x0, y0, z0) in enumerate(homes):
+            if at == pause:
+                then()
             member = (x0 * sizes[1] + y0) * sizes[2] + z0
             cell_at = corners(x0, y0, z0)
             held, store = stores[at % 2], stores[(at + 1) % 2]
@@ -484,12 +486,11 @@
             copy.start()
             backs.append(copy)
 
-    sums = across(sheet, sums)
-    give_back((1, 3, 5, 7))
     energy = lax.fori_loop(0, members, base_level, sums[0])
-    sums = energy, sums[1]
-    if border:
-        sums = across(border, sums)
+    far_side = functools.partial(give_back, (1, 3, 5, 7))
+    sums = across(sheet + border, (energy, sums[1]), len(sheet), far_side)
+    if not border:
+        far_side()
     part[0:1] = jnp.sum(sums[0], 0, keepdims=True)
     part[1:2] = jnp.sum(sums[1], 0, keepdims=True)
 
@@ -552,11 +553,9 @@
             forces[pl.ds(at, 1)] = value[axis : axis + 1]
     for copy in plane_copies:
         copy.wait()
-    summed = plane[0]
-    for step in range(1, count_plane):
-        summed = summed + plane[step]
-    totals[0] = jnp.sum(summed[0:1]) * normaliser
-    totals[1] = jnp.sum(summed[1:2]) * normaliser
+    summed = jnp.sum(plane[...], 0)
+    whole = jnp.sum(summed, 1, keepdims=True) * normaliser
+    totals[...] = jnp.broadcast_to(whole, totals.shape)
 
 
 def per_device(positions, type_ids, counts, type_charge, type_sigma, type_epsilon):
@@ -566,7 +565,6 @@
     cells = ext_sizes[0] * ext_sizes[1] * ext_sizes[2]
     members = sizes[0] * sizes[1] * sizes[2]
     vmem = pl.BlockSpec(memory_space=pltpu.VMEM)
-    smem = pl.BlockSpec(memory_space=pltpu.SMEM)
     hbm = pl.BlockSpec(memory_space=pltpu.HBM)
     f32 = jnp.float32
     count_x, count_y, count_z = (lax.axis_size(axis) for axis in AXES)
@@ -598,10 +596,10 @@
         name="step",
         out_shape=(
             jax.ShapeDtypeStruct((3 * members, width), f32),
-            jax.ShapeDtypeStruct((2,), f32),
+            jax.ShapeDtypeStruct((2, width), f32),
         ),
         in_specs=[hbm] * 6,
-        out_specs=(vmem, smem),
+        out_specs=(vmem, vmem),
         scratch_shapes=[
             pltpu.SMEM((types,), f32),
             pltpu.SMEM((types,), f32),
@@ -642,7 +640,7 @@
             collective_id=0, has_side_effects=True, vmem_limit_bytes=VMEM_LIMIT
         ),
     )(type_charge, type_sigma, type_epsilon, positions, type_ids, counts)
-    return forces.reshape((3,) + sizes + (width,)), totals
+    return forces.reshape((3,) + sizes + (width,)), totals[:, 0]
 
 
 def solution(mesh):

time: 37.8 us -> 37.4 us (0.989)
  Pallas kernels: 35.9 us -> 35.3 us
    slice x0 -> x1, local copies, waits for them, and re-layouts: none -> 0.63 us  [per_device(): return (forces.reshape((3,) + sizes + (width,)), totals[:, 0])]
    pallas_call x1, Pallas kernels: 35.9 us -> 35.3 us  [per_device(): pl.pallas_call(functools.partial(step_kernel, normaliser, types), name='s...]
    unnamed x2 -> x1, local copies, waits for them, and re-layouts: 1.12 us -> 0.61 us
where the time goes in v7:
time: 37.4 us; the launch traced here: 37.2 us
  Pallas kernels  35.3 us (94%)
  local copies, waits for them, and re-layouts  1.23 us (3%)
  between operations  0.64 us (2%)
    pallas_call x1, Pallas kernels, per_device(): pl.pallas_call(functools.partial(step_kernel, normaliser, types), name='s...  35.3 us

profile of v7, /device:TPU:0, one launch (start us, length us, event | category | flops | bytes accessed | tf_op | source)
XLA Modules:
  0.0 37.2 jit_solution(3194142270496528257)
XLA Ops:
  0.6 35.3 %step.1 = (f32[48,128]{1,0:T(8,128)S(1)}, f32[2,128]{1,0:T(2,128)S(1)}) custom-call(f32[2]{0:T(128)} %charge_all.1, f32[2]{0:T(128)} %sigma_all.1, f32[2]{0:T(128)} %epsilon_all.1, f32[3,2,4,2,128]{4,3,2,1,0:T(2,128)} %positions.1, s32[2,4,2,128]{3,2,1,0:T(2,128)} %type_ids.1, s32[2,2,4]{2,1,0:T(2,128)} %bitcast.3), custom_call_target="tpu_custom_call" | custom-call | tf_op jit(solution)/shard_map/step/pallas_call | solution.py:594
  35.9 0.6 %slice_reduce_fusion = f32[2]{0:T(128)} fusion(f32[2,128]{1,0:T(2,128)S(1)} %get-tuple-element.5), kind=kLoop, calls=%fused_computation | loop fusion | bytes 16 | tf_op jit(solution)/shard_map/slice | solution.py:643
  36.6 0.6 %copy.9 = f32[3,2,4,2,128]{4,3,2,1,0:T(2,128)} copy(f32[3,2,4,2,128]{4,3,2,1,0:T(2,128)S(1)} %bitcast.2) | data formatting | bytes 49152
